TPU v7x, 256 devices: a whole 4x4x8 slice. The times are simulated.
256 devices in a mesh: dp: 16 (over y, x_hi, core), space: 16 (over x_lo, z).
Axes of the slice: x: 4 (x_hi: 2, x_lo: 2; x = x_hi * 2 + x_lo), y: 4, z: 8, core: 2. Of those that a mesh axis runs over, the one named last changes fastest.
Arguments:
- act_in: bfloat16 [16, 32, 64, 2048], P('dp', 'space'), may hold values from -6 to 6
- weight_one: bfloat16 [3, 3, 3, 32, 64], replicated, may hold values from -0.21875 to 0.21875
- bias_one: float32 [64], replicated, may hold values from -3 to 3
- weight_two: bfloat16 [3, 3, 3, 64, 128], replicated, may hold values from -0.15625 to 0.15625
- bias_two: float32 [128], replicated, may hold values from -3 to 3
- cotangent: bfloat16 [16, 16, 32, 4096], P('dp', 'space'), may hold values from -24 to 24
Outputs:
- grad_input: bfloat16 [16, 32, 64, 2048], P('dp', 'space')
- grad_w_one: float32 [3, 3, 3, 32, 64], replicated
- grad_b_one: float32 [64], replicated
- grad_w_two: float32 [3, 3, 3, 64, 128], replicated
- grad_b_two: float32 [128], replicated
All inputs are finite; a program needn't handle non-finite values.
Results may differ from a plain program's by a relative error of at most 0.01.
Values may be sent and summed in bfloat16 or wider, within the bound.
A program may use at most 128 MiB of HBM per device.

v0:
```python
import math

import jax
import jax.numpy as jnp
from jax import lax
from jax.sharding import PartitionSpec as P


def padded_2(cells, sides, width):
    for axis, dim in sides:
        count = lax.axis_size(axis)
        ends = count - 1
        head = lax.slice_in_dim(cells, 0, width, axis=dim)
        tail = lax.slice_in_dim(cells, cells.shape[dim] - width, cells.shape[dim], axis=dim)
        cells = jnp.concatenate(
            [
                lax.ppermute(tail, axis, [(i, (i + 1) % count) for i in range(ends)]),
                cells,
                lax.ppermute(head, axis, [((i + 1) % count, i) for i in range(ends)]),
            ],
            axis=dim,
        )
    return cells


def forward_conv(padded, kernel):
    return lax.conv_general_dilated(
        padded,
        kernel,
        (1, 1, 1),
        ((0, 0), (1, 1), (1, 1)),
        dimension_numbers=("NDHWC", "DHWIO", "NDHWC"),
        preferred_element_type=jnp.float32,
    )


def weight_grad(padded, delta):
    return lax.conv_general_dilated(
        padded,
        delta,
        (1, 1, 1),
        ((0, 0), (1, 1), (1, 1)),
        dimension_numbers=("CDHWN", "IDHWO", "DHWNC"),
        preferred_element_type=jnp.float32,
    )


def input_grad(delta, kernel, depth_pad):
    return lax.conv_general_dilated(
        delta,
        kernel[::-1, ::-1, ::-1],
        (1, 1, 1),
        (depth_pad, (1, 1), (1, 1)),
        dimension_numbers=("NDHWC", "DHWOI", "NDHWC"),
        preferred_element_type=jnp.float32,
    )


def silu_slope(value):
    sig = jax.nn.sigmoid(value)
    return sig * (1.0 + value * (1.0 - sig))


def local(act_in, weight_one, bias_one, weight_two, bias_two, cotangent):
    samples, slab, side, merged = act_in.shape
    chan_in = weight_one.shape[3]
    chan_mid = weight_one.shape[4]
    chan_out = weight_two.shape[4]
    half = side // 2
    slab_two = slab // 2
    batch_all = samples * lax.axis_size("dp")
    depth_all = slab * lax.axis_size("space")
    scale_one = 16.0 / math.sqrt(batch_all * depth_all * side * side)
    scale_two = 1.0 / math.sqrt(batch_all * (depth_all // 2) * half * half)
    x_pad = padded_2(act_in, (("space", 1),), 1).reshape(samples, slab + 2, side, side, chan_in)
    pre_one = forward_conv(x_pad, weight_one) + bias_one
    act_one = pre_one * jax.nn.sigmoid(pre_one)
    pooled = (
        act_one.reshape(samples, slab_two, 2, half, 2, half, 2, chan_mid)
        .mean(axis=(2, 4, 6))
        .astype(jnp.bfloat16)
    )
    pool_pad = padded_2(
        pooled.reshape(samples, slab_two, half, half * chan_mid), (("space", 1),), 1
    ).reshape(samples, slab_two + 2, half, half, chan_mid)
    pre_two = forward_conv(pool_pad, weight_two) + bias_two
    cot_five = cotangent.reshape(samples, slab_two, half, half, chan_out)
    delta_two = (cot_five.astype(jnp.float32) * silu_slope(pre_two)).astype(jnp.bfloat16)
    gw_two = weight_grad(pool_pad, delta_two)
    gb_two = jnp.sum(delta_two, axis=(0, 1, 2, 3), dtype=jnp.float32)
    gw_two, gb_two = lax.psum((gw_two, gb_two), ("dp", "space"))
    delta_pad = padded_2(
        delta_two.reshape(samples, slab_two, half, half * chan_out), (("space", 1),), 1
    ).reshape(samples, slab_two + 2, half, half, chan_out)
    grad_pooled = input_grad(delta_pad, weight_two, (0, 0))
    spread = jnp.broadcast_to(
        grad_pooled[:, :, None, :, None, :, None, :],
        (samples, slab_two, 2, half, 2, half, 2, chan_mid),
    ).reshape(samples, slab, side, side, chan_mid)
    delta_one = (spread / 8.0 * silu_slope(pre_one)).astype(jnp.bfloat16)
    gw_one = weight_grad(x_pad, delta_one)
    gb_one = jnp.sum(delta_one, axis=(0, 1, 2, 3), dtype=jnp.float32)
    delta_one_pad = padded_2(
        delta_one.reshape(samples, slab, side, side * chan_mid), (("space", 1),), 1
    ).reshape(samples, slab + 2, side, side, chan_mid)
    grad_x = input_grad(delta_one_pad, weight_one, (0, 0))
    gw_one, gb_one = lax.psum((gw_one, gb_one), ("dp", "space"))
    grad_input = grad_x.astype(jnp.bfloat16).reshape(samples, slab, side, side * chan_in)
    return (
        grad_input,
        gw_one * scale_one,
        gb_one * scale_one,
        gw_two * scale_two,
        gb_two * scale_two,
    )


def solution(mesh):
    placed = (P("dp", "space", None, None), P(), P(), P(), P(), P("dp", "space", None, None))
    return jax.shard_map(
        local,
        mesh=mesh,
        in_specs=placed,
        out_specs=(P("dp", "space", None, None), P(), P(), P(), P()),
        check_vma=False,
    )
```

profile of v0, /device:TPU:1, one launch (start us, length us, event | category | flops | bytes accessed | tf_op | source)
XLA Modules:
  0.0 471.9 jit_solution(11770701972416479829)
XLA Ops:
  7.2 1.6 copy.175
  8.9 4.4 collective-permute-start
  13.3 1.3 collective-permute-start.1
  14.6 9.3 %collective-permute-done = bf16[1,1,64,2048]{2,3,1,0:T(8,128)(2,1)S(1)} collective-permute-done((bf16[1,1,64,2048]{2,3,1,0:T(8,128)(2,1)S(1)}, bf16[1,1,64,2048]{2,3,1,0:T(8,128)(2,1)S(1)}, u32[]{:S(2)}, u32[]{:S(2)}) %collective-permute-start) | collective-permute-done | bytes 262176 | tf_op jit(solution)/shard_map/ppermute | solution.py:17
  23.8 4.2 collective-permute-done.1
  28.0 1.7 pad_maximum_fusion
  29.7 1.9 pad
  31.7 6.7 %copy.179 = bf16[4,64,1,8,9,32]{5,3,4,1,0,2:T(8,128)(2,1)} copy(bf16[4,64,1,8,9,32]{1,5,4,3,0,2:T(8,128)(2,1)} %bitcast.114) | data formatting | bytes 2359296 | tf_op jit(solution)/shard_map/conv_general_dilated | solution.py:27
  38.4 1.5 slice.27
  40.0 11.3 %fusion.16 = (f32[2,64,8,9,64]{4,2,3,1,0:T(8,128)S(1)}, f32[2,64,8,9,64]{4,2,3,1,0:T(8,128)}) fusion(f32[64]{0:T(128)S(1)} %copy-done.9, pred[8,9]{0,1:T(8,128)(4,1)S(1)} %copy-done.11, bf16[3,3,3,32,64]{4,3,2,1,0:T(8,128)(2,1)S(1)} %copy-done.7, bf16[4,64,1,7,2,32]{5,3,4,1,0,2:T(8,128)(2,1)S(1)} %slice.27, bf16[4,64,1,8,9,32]{5,3,4,1,0,2:T(8,128)(2,1)} %copy.179), kind=kOutput, calls=%fused_computation.18 | convolution fusion | flops 1018822656 | bytes 6238536 | tf_op jit(solution)/shard_map/conv_general_dilated | solution.py:27
  51.3 0.9 copy.180
  52.2 2.0 slice_reduce_fusion
  54.2 3.3 reduce_sum.36
  57.9 4.2 collective-permute-start.2
  62.3 1.5 collective-permute-start.3
  63.8 5.5 %copy.198 = f32[2,64,8,9,64]{4,1,3,2,0:T(8,128)} copy(f32[2,64,8,9,64]{4,2,3,1,0:T(8,128)} %get-tuple-element.42) | data formatting | bytes 4718592 | tf_op jit(solution)/shard_map/mul | solution.py:61
  69.3 13.0 %copy.205 = bf16[1,4,64,64,32]{4,0,3,2,1:T(2,128)(2,1)} copy(bf16[1,4,64,64,32]{2,4,3,1,0:T(8,128)(2,1)S(1)} %bitcast.106) | data formatting | bytes 2097152 | tf_op jit(solution)/shard_map/reshape | solution.py:75
  82.3 1.2 concatenate.41
  84.7 1.2 concatenate.42
  86.6 0.9 copy.236
  88.2 1.5 add_multiply_fusion.1
  89.9 0.8 convert_reduce_fusion.1
  90.8 4.9 %collective-permute-start.4 = (bf16[1,1,32,4096]{3,2,1,0:T(8,128)(2,1)S(1)}, bf16[1,1,32,4096]{3,2,1,0:T(8,128)(2,1)S(1)}, u32[]{:S(2)}, u32[]{:S(2)}) collective-permute-start(bf16[1,1,32,4096]{3,2,1,0:T(8,128)(2,1)S(1)} %reshape.106), channel_id=1, source_target_pairs={{0,1},{1,2},{2,3},{3,4},{4,5},{5,6},{6,7},{7,8},{8,9},{9,10},{10,1... | collective-permute-start | bytes 786440 | tf_op jit(solution)/shard_map/ppermute | solution.py:17
  95.7 1.7 collective-permute-start.5
  97.4 8.1 %fusion.56 = f32[3,3,3,64,128]{4,3,2,1,0:T(8,128)} fusion(bf16[1,3,32,32,64]{4,0,3,2,1:T(2,128)(2,1)S(1)} %constant_dynamic-update-slice_fusion, bf16[1,1,32,32,128]{4,3,1,2,0:T(8,128)(2,1)S(1)} %get-tuple-element.40), kind=kOutput, calls=%fused_computation.65 | convolution fusion | flops 434307072 | bytes 1540096 | tf_op jit(solution)/shard_map/conv_general_dilated | solution.py:38
  106.6 2.5 fusion.47
  109.3 1.0 broadcast_in_dim.4
  111.1 1.4 copy-done.2
  112.5 1.5 copy.238
  114.0 2.5 reshape.107
  116.5 2.3 fusion.71
  118.8 5.7 %collective-permute-start.6 = (bf16[1,1,64,4096]{3,2,1,0:T(8,128)(2,1)}, bf16[1,1,64,4096]{3,2,1,0:T(8,128)(2,1)}, u32[]{:S(2)}, u32[]{:S(2)}) collective-permute-start(bf16[1,1,64,4096]{3,2,1,0:T(8,128)(2,1)} %get-tuple-element.45), channel_id=1, source_target_pairs={{0,1},{1,2},{2,3},{3,4},{4,5},{5,6},{6,7},{7,8},{8,9},{9,10},{10,1... | collective-permute-start | bytes 1572872 | tf_op jit(solution)/shard_map/ppermute | solution.py:17
  124.5 1.3 collective-permute-start.7
  125.8 66.2 %fusion.18 = f32[3,3,3,32,64]{4,3,2,1,0:T(8,128)} fusion(bf16[1,4,64,64,32]{4,0,3,2,1:T(2,128)(2,1)} %copy.205, bf16[1,2,64,64,64]{4,3,2,1,0:T(8,128)(2,1)S(1)} %bitcast.108), kind=kOutput, calls=%fused_computation.25 | convolution fusion | flops 887193600 | bytes 2318336 | tf_op jit(solution)/shard_map/conv_general_dilated | solution.py:38
  192.0 2.8 convert_reduce_fusion
  194.8 83.0 %all-reduce = (f32[64]{0:T(128)S(1)}, f32[128]{0:T(128)S(1)}) all-reduce(f32[64]{0:T(128)S(1)} %convert_reduce_fusion, f32[128]{0:T(128)S(1)} %copy-done.6), channel_id=1, replica_groups=mesh['dp'=16,'space'=16] {'dp','space'}, use_global_device_ids=true, to_apply=%region_4.0 | all-reduce | flops 192 | bytes 1536 | tf_op jit(solution)/shard_map/psum | solution.py:107
  278.9 2.8 concatenate.34
  281.7 2.8 concatenate.35
  284.4 2.2 maximum_bitcast_fusion
  286.7 2.7 copy.213
  289.4 1.3 pad.6.clone
  290.7 3.0 copy.203
  294.0 18.1 %fusion.4 = bf16[2,64,8,9,32]{4,2,3,1,0:T(8,128)(2,1)} fusion(bf16[3,3,3,32,64]{4,3,2,1,0:T(8,128)(2,1)S(1)} %copy-done.8, bf16[4,64,1,7,2,64]{5,3,4,1,0,2:T(8,128)(2,1)S(1)} %slice.36, bf16[4,64,1,8,9,64]{5,3,4,1,0,2:T(8,128)(2,1)S(1)} %copy.203), kind=kOutput, calls=%fused_computation.6 | convolution fusion | flops 1017249792 | bytes 3518464 | tf_op jit(solution)/shard_map/conv_general_dilated | solution.py:49
  312.1 3.2 copy.204
  315.7 1.1 copy.208
  316.9 143.7 %all-reduce.4.cloned.1.call-done = (f32[3,3,3,32,64]{4,3,2,1,0:T(8,128)}, f32[3,3,3,64,128]{4,3,2,1,0:T(8,128)}) async-done(((f32[3,3,3,32,64]{4,3,2,1,0:T(8,128)}, f32[3,3,3,64,128]{4,3,2,1,0:T(8,128)}), (f32[3,3,3,32,64]{4,3,2,1,0:T(8,128)}, f32[3,3,3,64,128]{4,3,2,1,0:T(8,128)})) %all-reduce.4.cloned.1.call-update) | async-done | bytes 1105936 | tf_op jit(solution)/shard_map/psum | solution.py:107
  460.6 2.2 broadcast_multiply_fusion
  462.8 1.8 broadcast_multiply_fusion.1
  (68 shorter events, 7.1 us)
Async XLA Ops:
  7.2 81.0 %copy-start = (bf16[3,3,3,64,128]{4,3,2,1,0:T(8,128)(2,1)S(1)}, bf16[3,3,3,64,128]{4,3,2,1,0:T(8,128)(2,1)}, u32[]{:S(2)}) copy-start(bf16[3,3,3,64,128]{4,3,2,1,0:T(8,128)(2,1)} %param.9) | copy-start | bytes 1327108
  7.2 453.4 %all-reduce.4.cloned.1.call-start = ((), (), s32[]{:S(2)}) async-start(), calls=%async_computation | async-start | bytes 2654208 | tf_op jit(solution)/shard_map/psum | solution.py:107
  8.8 15.0 %copy-start.3 = (bf16[1,2,64,2048]{2,3,1,0:T(8,128)(2,1)}, bf16[1,2,64,2048]{2,3,1,0:T(8,128)(2,1)S(1)}, u32[]{:S(2)}) copy-start(bf16[1,2,64,2048]{2,3,1,0:T(8,128)(2,1)S(1)} %copy.175) | copy-start | bytes 1572868
  8.9 15.0 %collective-permute-start = (bf16[1,1,64,2048]{2,3,1,0:T(8,128)(2,1)S(1)}, bf16[1,1,64,2048]{2,3,1,0:T(8,128)(2,1)S(1)}, u32[]{:S(2)}, u32[]{:S(2)}) collective-permute-start(bf16[1,1,64,2048]{2,3,1,0:T(8,128)(2,1)S(1)} %get-tuple-element.47), channel_id=1, source_target_pairs={{0,1},{1,2},{2,3},{3,4},{4,5},{5,6},{6,7},{7,8},{8,9},{9,10},{10,1... | collective-permute-start | bytes 786440 | tf_op jit(solution)/shard_map/ppermute | solution.py:17
  13.3 14.7 %collective-permute-start.1 = (bf16[1,1,64,2048]{2,3,1,0:T(8,128)(2,1)S(1)}, bf16[1,1,64,2048]{2,3,1,0:T(8,128)(2,1)S(1)}, u32[]{:S(2)}, u32[]{:S(2)}) collective-permute-start(bf16[1,1,64,2048]{2,3,1,0:T(8,128)(2,1)S(1)} %get-tuple-element.48), channel_id=1, source_target_pairs={{1,0},{2,1},{3,2},{4,3},{5,4},{6,5},{7,6},{8,7},{9,8},{10,9},{11,1... | collective-permute-start | bytes 786440 | tf_op jit(solution)/shard_map/ppermute | solution.py:19
  31.7 8.3 %copy-start.7 = (bf16[3,3,3,32,64]{4,3,2,1,0:T(8,128)(2,1)S(1)}, bf16[3,3,3,32,64]{4,3,2,1,0:T(8,128)(2,1)}, u32[]{:S(2)}) copy-start(bf16[3,3,3,32,64]{4,3,2,1,0:T(8,128)(2,1)} %param.7) | copy-start | bytes 331780
  31.7 8.3 %copy-start.9 = (f32[64]{0:T(128)S(1)}, f32[64]{0:T(128)}, u32[]{:S(2)}) copy-start(f32[64]{0:T(128)} %param.8) | copy-start | bytes 772
  31.7 8.3 %copy-start.11 = (pred[8,9]{0,1:T(8,128)(4,1)S(1)}, pred[8,9]{0,1:T(8,128)(4,1)}, u32[]{:S(2)}) copy-start(pred[8,9]{0,1:T(8,128)(4,1)} %constant.38) | copy-start | bytes 220
  52.2 10.0 %copy-start.4 = (bf16[1,1,32,4096]{3,2,1,0:T(8,128)(2,1)S(1)}, bf16[1,1,32,4096]{3,2,1,0:T(8,128)(2,1)}, u32[]{:S(2)}) copy-start(bf16[1,1,32,4096]{3,2,1,0:T(8,128)(2,1)} %param.11) | copy-start | bytes 786436
  57.9 24.4 %collective-permute-start.2 = (bf16[1,1,32,2048]{3,2,1,0:T(8,128)(2,1)S(1)}, bf16[1,1,32,2048]{3,2,1,0:T(8,128)(2,1)}, u32[]{:S(2)}, u32[]{:S(2)}) collective-permute-start(bf16[1,1,32,2048]{3,2,1,0:T(8,128)(2,1)S(1)} %convert_element_type.57), channel_id=1, source_target_pairs={{0,1},{1,2},{2,3},{3,4},{4,5},{5,6},{6,7},{7,8},{8,9},{9,10},{10,1... | collective-permute-start | bytes 393224 | tf_op jit(solution)/shard_map/ppermute | solution.py:17
  62.3 22.4 %collective-permute-start.3 = (bf16[1,1,32,2048]{3,2,1,0:T(8,128)(2,1)S(1)}, bf16[1,1,32,2048]{3,2,1,0:T(8,128)(2,1)}, u32[]{:S(2)}, u32[]{:S(2)}) collective-permute-start(bf16[1,1,32,2048]{3,2,1,0:T(8,128)(2,1)S(1)} %convert_element_type.57), channel_id=1, source_target_pairs={{1,0},{2,1},{3,2},{4,3},{5,4},{6,5},{7,6},{8,7},{9,8},{10,9},{11,1... | collective-permute-start | bytes 393224 | tf_op jit(solution)/shard_map/ppermute | solution.py:19
  84.7 3.5 copy-start.10
  84.7 3.5 copy-start.12
  90.8 14.6 %collective-permute-start.4 = (bf16[1,1,32,4096]{3,2,1,0:T(8,128)(2,1)S(1)}, bf16[1,1,32,4096]{3,2,1,0:T(8,128)(2,1)S(1)}, u32[]{:S(2)}, u32[]{:S(2)}) collective-permute-start(bf16[1,1,32,4096]{3,2,1,0:T(8,128)(2,1)S(1)} %reshape.106), channel_id=1, source_target_pairs={{0,1},{1,2},{2,3},{3,4},{4,5},{5,6},{6,7},{7,8},{8,9},{9,10},{10,1... | collective-permute-start | bytes 786440 | tf_op jit(solution)/shard_map/ppermute | solution.py:17
  95.7 9.8 %collective-permute-start.5 = (bf16[1,1,32,4096]{3,2,1,0:T(8,128)(2,1)S(1)}, bf16[1,1,32,4096]{3,2,1,0:T(8,128)(2,1)S(1)}, u32[]{:S(2)}, u32[]{:S(2)}) collective-permute-start(bf16[1,1,32,4096]{3,2,1,0:T(8,128)(2,1)S(1)} %reshape.106), channel_id=1, source_target_pairs={{1,0},{2,1},{3,2},{4,3},{5,4},{6,5},{7,6},{8,7},{9,8},{10,9},{11,1... | collective-permute-start | bytes 786440 | tf_op jit(solution)/shard_map/ppermute | solution.py:19
  106.5 3.8 slice-start
  106.6 3.7 slice-start.1
  111.1 1.4 copy-start.2
  118.8 160.1 %collective-permute-start.6 = (bf16[1,1,64,4096]{3,2,1,0:T(8,128)(2,1)}, bf16[1,1,64,4096]{3,2,1,0:T(8,128)(2,1)}, u32[]{:S(2)}, u32[]{:S(2)}) collective-permute-start(bf16[1,1,64,4096]{3,2,1,0:T(8,128)(2,1)} %get-tuple-element.45), channel_id=1, source_target_pairs={{0,1},{1,2},{2,3},{3,4},{4,5},{5,6},{6,7},{7,8},{8,9},{9,10},{10,1... | collective-permute-start | bytes 1572872 | tf_op jit(solution)/shard_map/ppermute | solution.py:17
  124.5 157.2 %collective-permute-start.7 = (bf16[1,1,64,4096]{3,2,1,0:T(8,128)(2,1)}, bf16[1,1,64,4096]{3,2,1,0:T(8,128)(2,1)}, u32[]{:S(2)}, u32[]{:S(2)}) collective-permute-start(bf16[1,1,64,4096]{3,2,1,0:T(8,128)(2,1)} %get-tuple-element.46), channel_id=1, source_target_pairs={{1,0},{2,1},{3,2},{4,3},{5,4},{6,5},{7,6},{8,7},{9,8},{10,9},{11,1... | collective-permute-start | bytes 1572872 | tf_op jit(solution)/shard_map/ppermute | solution.py:19
  125.7 69.1 %copy-start.6 = (f32[128]{0:T(128)S(1)}, f32[128]{0:T(128)}, u32[]{:S(2)}) copy-start(f32[128]{0:T(128)} %get-tuple-element.39) | copy-start | bytes 1540
  290.7 3.3 copy-start.8
  294.0 21.3 %copy-start.5 = (pred[8,9]{1,0:T(8,128)(4,1)S(1)}, pred[8,9]{1,0:T(8,128)(4,1)}, u32[]{:S(2)}) copy-start(pred[8,9]{1,0:T(8,128)(4,1)} %constant.34) | copy-start | bytes 220
  312.1 152.5 %copy-start.1 = (bf16[3,3,3,64,128]{4,3,2,1,0:T(8,128)(2,1)S(1)}, bf16[3,3,3,64,128]{4,3,2,1,0:T(8,128)(2,1)}, u32[]{:S(2)}) copy-start(bf16[3,3,3,64,128]{4,3,2,1,0:T(8,128)(2,1)} %param.9) | copy-start | bytes 1327108
Sparse Core Ops, SparseCore 0:
  194.9 265.5 all-reduce.3
where the time goes:
time: 481 us; the launch traced here: 472 us
  waiting for transfers between devices  157 us (33%)
  matrix products  108 us (22%)
  blocking collectives  83 us (17%)
  local copies, waits for them, and re-layouts  64.9 us (13%)
  starting transfers between devices  25 us (5%)
  other arithmetic  19.1 us (4%)
  between operations  15 us (3%)
    psum x1, waiting for transfers between devices, local(): gw_one, gb_one = lax.psum((gw_one, gb_one), ('dp', 'space'))  144 us
    psum x1, blocking collectives, local(): gw_one, gb_one = lax.psum((gw_one, gb_one), ('dp', 'space'))  83 us
    conv_general_dilated x2, matrix products, weight_grad(): lax.conv_general_dilated(padded, delta, (1, 1, 1), ((0, 0), (1, 1), (1, 1...  74.3 us
    conv_general_dilated x2, matrix products, input_grad(): lax.conv_general_dilated(delta, kernel[::-1, ::-1, ::-1], (1, 1, 1), (dep...  20.6 us
    ppermute x4, starting transfers between devices, padded_2(): lax.ppermute(tail, axis, [(i, (i + 1) % count) for i in range(ends)])  19.2 us
    reshape x2, local copies, waits for them, and re-layouts, local(): padded_2(act_in, (('space', 1),), 1)  15 us
    conv_general_dilated x2, matrix products, forward_conv(): lax.conv_general_dilated(padded, kernel, (1, 1, 1), ((0, 0), (1, 1), (1,...  12.8 us
    concatenate x8, local copies, waits for them, and re-layouts, padded_2(): jnp.concatenate([lax.ppermute(tail, axis, [(i, (i + 1) % count) for i in...  10.2 us
  transfers between devices with their start and end apart: 9, of which 3 were waited for; matrix products, arithmetic and copies ran while one was open for 29% of the time, Pallas kernels for 0%

commit v1 on v0

v1 whole, which is shorter than its diff:
```python
import functools
import math

import jax
import jax.numpy as jnp
from jax import lax
from jax.experimental import pallas as pl
from jax.experimental.pallas import tpu as pltpu
from jax.sharding import PartitionSpec as P

F32 = jnp.float32
BF16 = jnp.bfloat16
LINK = jnp.float32
MESH = pl.DeviceIdType.MESH

E0, O0, EP, OM = 0, 1, 2, 3
FWD = ((OM, E0, O0), (E0, O0, EP))
BWD = ((O0, E0, OM), (EP, O0, E0))

NT = (((1,), (1,)), ((), ()))
TN = (((0,), (0,)), ((), ()))


def dot(a, b):
    return jnp.dot(a, b, preferred_element_type=F32)


def slope_of(value, sig):
    return sig * (1.0 + value * (1.0 - sig))


def sigmoid(value):
    return 0.5 * jnp.tanh(0.5 * value) + 0.5


def kernel(
    scale_one, scale_two,
    x_ref, w1_ref, b1_ref, w2_ref, b2_ref, cot_ref,
    gx_ref, gw1_ref, gb1_ref, gw2_ref, gb2_ref,
    t1, t2, xf, xv, halo_x, slope, pf, pool, halo_p, ps, d2, gsend, grecv, gown, gp,
    d1, d1t, xsend, xrecv, xown, outf,
    acc, r0, half, r1, r2, final,
    s_send, s_recv, a_send, a_recv, z_send, z_recv, g_send, g_recv, c_send, c_recv,
):
    dp = lax.axis_index("dp")
    space = lax.axis_index("space")
    nxt = lax.rem(space + 1, 16)
    prv = lax.rem(space + 15, 16)
    core = lax.rem(dp, 2)
    x_pos = lax.rem(dp // 2, 2) * 2 + space // 8
    chip = (dp // 4) * 4 + x_pos
    z = lax.rem(space, 8)
    partner = (dp + 1 - 2 * core, space)

    def chip_at(r):
        q = lax.rem(chip + r, 16)
        qx = lax.rem(q, 4)
        return (q // 4) * 4 + (qx // 2) * 2 + core, lax.rem(qx, 2) * 8 + z, q

    def z_at(r):
        return dp, (space // 8) * 8 + lax.rem(z + r, 8)

    barrier = pltpu.get_barrier_semaphore()

    def greet(device):
        pl.semaphore_signal(barrier, inc=1, device_id=device, device_id_type=MESH)

    greet((dp, nxt))
    greet((dp, prv))
    greet(partner)
    for r in range(1, 16):
        greet(chip_at(r)[:2])
    for r in range(1, 8):
        greet(z_at(r))

    for k in range(3):
        for j in range(3):
            w = w1_ref[k, j].reshape(96, 64).astype(F32)
            for t in range(2):
                cols = []
                for v in (t, t + 2):
                    parts = [w]
                    if v:
                        parts = [jnp.zeros((32 * v, 64), F32)] + parts
                    parts = parts + [jnp.zeros((160 - 32 * v, 64), F32)]
                    cols.append(jnp.concatenate(parts, axis=0))
                t1[pl.ds((k * 3 + j) * 256, 256), pl.ds(t * 128, 128)] = jnp.concatenate(cols, axis=1).astype(BF16)
            w = w2_ref[k, j].reshape(192, 128)
            gap = jnp.zeros((64, 128), BF16)
            t2[pl.ds((k * 3 + j) * 256, 256), pl.ds(0, 128)] = jnp.concatenate([w, gap], axis=0)
            t2[pl.ds((k * 3 + j) * 256, 256), pl.ds(128, 128)] = jnp.concatenate([gap, w], axis=0)

    pl.semaphore_wait(barrier, 25)

    def exchange(down, up, from_next, from_prev, stage):
        one = pltpu.make_async_remote_copy(
            src_ref=down, dst_ref=from_next, send_sem=s_send.at[stage, 0], recv_sem=s_recv.at[stage, 0],
            device_id=(dp, prv), device_id_type=MESH)
        two = pltpu.make_async_remote_copy(
            src_ref=up, dst_ref=from_prev, send_sem=s_send.at[stage, 1], recv_sem=s_recv.at[stage, 1],
            device_id=(dp, nxt), device_id_type=MESH)
        one.start()
        two.start()
        return one, two

    def finish(pair):
        pair[0].wait()
        pair[1].wait()

    not_last = space < 15
    not_first = space > 0

    pair = exchange(x_ref.at[0, 0], x_ref.at[0, 1], halo_x.at[1], halo_x.at[0], 0)

    xf[:, 0:8, :] = jnp.zeros((17, 8, 128), F32)
    xf[:, 72:80, :] = jnp.zeros((17, 8, 128), F32)
    lane = lax.broadcasted_iota(jnp.int32, (16, 128), 1)

    def prepare(src, plane, keep):
        def rows(i, carry):
            v = src[pl.ds(pl.multiple_of(i * 16, 16), 16), :].astype(F32)
            if keep is not None:
                v = jnp.where(keep, v, 0.0)
            v = pltpu.roll(v, 32, 1)
            at = pl.ds(pl.multiple_of(i * 16 + 8, 8), 16)
            xf[0, at, :] = jnp.where(lane < 32, 0.0, v[:, 0:128])
            for t in range(1, 16):
                xf[t, at, :] = v[:, t * 128:t * 128 + 128]
            xf[16, at, :] = jnp.where(lane < 32, v[:, 0:128], 0.0)
            return carry
        lax.fori_loop(0, 4, rows, 0)

        def tiles(i, carry):
            at = pl.ds(pl.multiple_of(i * 128, 128), 128)
            xv[plane, E0, :, at] = xf[i, pl.ds(8, 32, stride=2), :].astype(BF16)
            xv[plane, O0, :, at] = xf[i, pl.ds(9, 32, stride=2), :].astype(BF16)
            xv[plane, EP, :, at] = xf[i, pl.ds(10, 32, stride=2), :].astype(BF16)
            xv[plane, OM, :, at] = xf[i, pl.ds(7, 32, stride=2), :].astype(BF16)
            return carry
        lax.fori_loop(0, 17, tiles, 0)

    prepare(x_ref.at[0, 0], 1, None)
    prepare(x_ref.at[0, 1], 2, None)
    finish(pair)
    prepare(halo_x.at[0], 0, not_first)
    prepare(halo_x.at[1], 3, not_last)

    bias = jnp.concatenate([b1_ref[...], b1_ref[...]], axis=1)
    bias = jnp.concatenate([bias, bias], axis=1)

    def forward_one(g, carry):
        sums = [None] * 4
        for d in range(2):
            for p in range(2):
                lhs = jnp.concatenate([
                    jnp.concatenate([
                        xv[d + k, FWD[p][j], :, pl.ds(pl.multiple_of((g * 4 + b) * 128, 128), 256)]
                        for b in range(4)], axis=0)
                    for k in range(3) for j in range(3)], axis=1)
                pre = dot(lhs, t1[...]) + bias
                sig = sigmoid(pre)
                act = pre * sig
                slope[d * 2 + p, pl.ds(pl.multiple_of(g * 128, 128), 128), :] = slope_of(pre, sig) * 0.125
                for b in range(4):
                    part = act[b * 32:b * 32 + 32, 0:128] + act[b * 32:b * 32 + 32, 128:256]
                    sums[b] = part if sums[b] is None else sums[b] + part
        for b in range(4):
            pool[:, pl.ds(pl.multiple_of((g * 4 + b) * 128, 128), 128)] = (sums[b] * 0.125).astype(BF16)
        return carry
    lax.fori_loop(0, 4, forward_one, 0)

    pair = exchange(pool, pool, halo_p.at[1], halo_p.at[0], 1)

    pf[0:8, :] = jnp.zeros((8, 2176), F32)
    pf[40:48, :] = jnp.zeros((8, 2176), F32)
    lane_p = lax.broadcasted_iota(jnp.int32, (32, 2048), 1)
    lane_q = lax.broadcasted_iota(jnp.int32, (32, 128), 1)

    def prepare_pool(src, plane, keep):
        v = src[...].astype(F32)
        if keep is not None:
            v = jnp.where(keep, v, 0.0)
        v = pltpu.roll(v, 64, 1)
        pf[8:40, 0:2048] = jnp.where(lane_p < 64, 0.0, v)
        pf[8:40, 2048:2176] = jnp.where(lane_q < 64, v[:, 0:128], 0.0)
        for j in range(3):
            ps[plane, j] = pf[7 + j:39 + j, :].astype(BF16)

    prepare_pool(pool, 1, None)
    finish(pair)
    prepare_pool(halo_p.at[0], 0, not_first)
    prepare_pool(halo_p.at[1], 2, not_last)

    row = lax.broadcasted_iota(jnp.int32, (32, 256), 0)
    bias_two = jnp.concatenate([b2_ref[...], b2_ref[...]], axis=1)

    def shift_up(v):
        return jnp.where(row < 31, pltpu.roll(v, 31, 0), 0.0)

    def shift_down(v):
        return jnp.where(row > 0, pltpu.roll(v, 1, 0), 0.0)

    def forward_two(g, total):
        lhs = jnp.concatenate([
            jnp.concatenate([
                ps[k, j, :, pl.ds(pl.multiple_of((g * 4 + b) * 128, 128), 256)] for b in range(4)], axis=0)
            for k in range(3) for j in range(3)], axis=1)
        pre = dot(lhs, t2[...]) + bias_two
        slp = slope_of(pre, sigmoid(pre))
        for b in range(4):
            at = pl.ds(pl.multiple_of((g * 4 + b) * 256, 256), 256)
            rows = pl.ds(pl.multiple_of((g * 4 + b) * 32, 32), 32)
            delta = (cot_ref[0, 0, :, at].astype(F32) * slp[b * 32:b * 32 + 32]).astype(BF16)
            wide = delta.astype(F32)
            d2[1, rows, :] = delta
            d2[0, rows, :] = shift_up(wide).astype(BF16)
            d2[2, rows, :] = shift_down(wide).astype(BF16)
            total = total + wide
        return total
    total_two = lax.fori_loop(0, 4, forward_two, jnp.zeros((32, 256), F32))

    def window_tiles(win, put):
        for t in range(17):
            piece = None
            if t < 16:
                piece = win[t * 32:t * 32 + 32, 0:128]
            if t > 0:
                other = win[t * 32 - 32:t * 32, 128:256]
                piece = other if piece is None else piece + other
            put(t, piece)

    lhs_two = jnp.concatenate([d2[0], d2[1], d2[2]], axis=1)
    for k in (0, 2, 1):
        rhs = jnp.concatenate([t2[pl.ds((k * 3 + j) * 256, 256), :] for j in range(3)], axis=1)
        win = lax.dot_general(lhs_two, rhs, NT, preferred_element_type=F32)
        if k == 1:
            def put(t, piece):
                gown[:, t * 128:t * 128 + 128] = piece
        else:
            def put(t, piece, k=k):
                gsend[k // 2, :, t * 128:t * 128 + 128] = piece.astype(BF16)
        window_tiles(win, put)
    pair = exchange(gsend.at[0], gsend.at[1], grecv.at[1], grecv.at[0], 2)

    for k in range(3):
        for j in range(3):
            lhs = jnp.concatenate([ps[k, j, :, b * 128:b * 128 + 256] for b in range(16)], axis=0)
            g = lax.dot_general(lhs, d2[1], TN, preferred_element_type=F32)
            acc_rows = g[0:192, 0:128] + g[64:256, 128:256]
            for part in range(8):
                tap = k * 3 + j
                first = tap * 192 + part * 24
                acc[first // 72, pl.ds(first % 72, 24), :] = acc_rows[part * 24:part * 24 + 24]

    finish(pair)
    v = gown[...]
    v = v + jnp.where(not_first, grecv[0].astype(F32), 0.0) + jnp.where(not_last, grecv[1].astype(F32), 0.0)
    v = pltpu.roll(v, 2176 - 64, 1)
    gp[...] = v[:, 0:2048]

    def delta_one(b, total):
        g = gp[:, pl.ds(pl.multiple_of(b * 128, 128), 128)]
        g = jnp.concatenate([g, g], axis=1)
        rows = pl.ds(pl.multiple_of(b * 32, 32), 32)
        for d in range(2):
            for p in range(2):
                delta = (g * slope[d * 2 + p, rows, :]).astype(BF16)
                wide = delta.astype(F32)
                d1[d, E0 if p == 0 else O0, rows, :] = delta
                if p == 0:
                    d1[d, EP, rows, :] = shift_up(wide).astype(BF16)
                else:
                    d1[d, OM, rows, :] = shift_down(wide).astype(BF16)
                total = total + wide
        return total
    total_one = lax.fori_loop(0, 16, delta_one, jnp.zeros((32, 256), F32))

    def window_one(terms, q):
        lhs = jnp.concatenate([d1[d, BWD[q][j]] for d, k in terms for j in range(3)], axis=1)
        rhs = jnp.concatenate([t1[pl.ds((k * 3 + j) * 256, 256), :] for d, k in terms for j in range(3)], axis=1)
        return lax.dot_general(lhs, rhs, NT, preferred_element_type=F32)

    for side, terms in ((0, ((0, 0),)), (1, ((1, 2),))):
        for q in range(2):
            def put(t, piece, side=side, q=q):
                xsend[side, q, :, t * 128:t * 128 + 128] = piece.astype(BF16)
            window_tiles(window_one(terms, q), put)
    pair = exchange(xsend.at[0], xsend.at[1], xrecv.at[1], xrecv.at[0], 3)

    for d in range(2):
        for p in range(2):
            for c in range(4):
                v = d1[d, p, pl.ds(c * 128, 128), :]
                d1t[:, pl.ds((d * 2 + p) * 512 + c * 128, 128)] = jnp.transpose(v)

    total = jnp.sum(total_one, axis=0, keepdims=True)
    total = total[:, 0:128] + total[:, 128:256]
    total = total + pltpu.roll(total, 64, 1)
    low = lax.broadcasted_iota(jnp.int32, (64, 128), 1)
    total_col = jnp.sum(
        jnp.where(low == lax.broadcasted_iota(jnp.int32, (64, 128), 0), total, 0.0), axis=1, keepdims=True)
    two = jnp.sum(total_two, axis=0, keepdims=True)
    two = jnp.broadcast_to(two[:, 0:128] + two[:, 128:256], (8, 128))
    for k in range(3):
        for j in range(3):
            tap = k * 3 + j
            rhs = jnp.concatenate([
                xv[d + k, FWD[p][j], :, b * 128:b * 128 + 256]
                for d in range(2) for p in range(2) for b in range(16)], axis=0)
            g = dot(d1t[...], rhs)
            s = g[0:64, 0:128] + pltpu.roll(g[128:192, 0:256], 256 - 32, 1)[:, 0:128]
            s = s + pltpu.roll(g[64:128, 0:256], 256 - 64, 1)[:, 0:128]
            s = s + pltpu.roll(g[192:256, 0:256], 256 - 96, 1)[:, 0:128]
            if tap == 0:
                s = jnp.where(low < 96, s, total_col)
            if tap == 1:
                extra = jnp.zeros((8, 128), F32)
                sub = lax.broadcasted_iota(jnp.int32, (8, 128), 0)
                for quarter in range(4):
                    moved = pltpu.roll(two, (96 - 32 * quarter) % 128, 1) if quarter != 3 else two
                    extra = jnp.where(sub == quarter, moved, extra)
                s = jnp.where(low < 96, s, jnp.concatenate([extra] * 8, axis=0))
            for part in range(8):
                first = 1728 + tap * 64 + part * 8
                acc[first // 72, pl.ds(first % 72, 8), :] = s[part * 8:part * 8 + 8]

    swap = pltpu.make_async_remote_copy(
        src_ref=acc.at[pl.ds((1 - core) * 16, 16)], dst_ref=r0, send_sem=c_send.at[0], recv_sem=c_recv.at[0],
        device_id=partner, device_id_type=MESH)
    swap.start()

    def own_planes(e, terms):
        for q in range(2):
            def put(t, piece, q=q):
                xown[e, q, :, t * 128:t * 128 + 128] = piece
            window_tiles(window_one(terms, q), put)
    own_planes(0, ((0, 1), (1, 0)))
    swap.wait()

    def add_half(i, carry):
        half[i] = (acc[core * 16 + i] + r0[i]).astype(LINK)
        return carry
    lax.fori_loop(0, 16, add_half, 0)
    sends = []
    for r in range(1, 16):
        a, b, q = chip_at(r)
        cp = pltpu.make_async_remote_copy(
            src_ref=half.at[q], dst_ref=r1.at[r - 1], send_sem=a_send.at[r - 1], recv_sem=a_recv.at[r - 1],
            device_id=(a, b), device_id_type=MESH)
        cp.start()
        sends.append(cp)
    own_planes(1, ((0, 2), (1, 1)))
    piece = half[chip].astype(F32)
    for r in range(1, 16):
        sends[r - 1].wait()
        piece = piece + r1[r - 1].astype(F32)
    r2[z] = piece.astype(LINK)
    sends = []
    for r in range(1, 8):
        cp = pltpu.make_async_remote_copy(
            src_ref=r2.at[z], dst_ref=r2.at[z], send_sem=z_send.at[r - 1], recv_sem=z_recv.at[r - 1],
            device_id=z_at(r), device_id_type=MESH)
        cp.start()
        sends.append(cp)

    finish(pair)
    for e in range(2):
        for q in range(2):
            halo = xrecv[e, q].astype(F32)
            v = xown[e, q] + jnp.where(not_first if e == 0 else not_last, halo, 0.0)
            v = pltpu.roll(v, 2176 - 32, 1)[:, 0:2048]
            for t in range(16):
                outf[t, pl.ds(q, 32, stride=2), :] = v[:, t * 128:t * 128 + 128]
        for t in range(16):
            gx_ref[0, e, :, t * 128:t * 128 + 128] = outf[t].astype(BF16)

    for cp in sends:
        cp.wait()
    piece = r2[0].astype(F32)
    for i in range(1, 8):
        piece = piece + r2[i].astype(F32)
    mine = core * 16 + chip
    final[mine] = piece.astype(LINK)
    sends = []
    for r in range(1, 16):
        a, b, q = chip_at(r)
        cp = pltpu.make_async_remote_copy(
            src_ref=final.at[mine], dst_ref=final.at[mine], send_sem=g_send.at[r - 1], recv_sem=g_recv.at[r - 1],
            device_id=(a, b), device_id_type=MESH)
        cp.start()
        sends.append(cp)
    for cp in sends:
        cp.wait()
    swap = pltpu.make_async_remote_copy(
        src_ref=final.at[pl.ds(core * 16, 16)], dst_ref=final.at[pl.ds(core * 16, 16)],
        send_sem=c_send.at[1], recv_sem=c_recv.at[1], device_id=partner, device_id_type=MESH)
    swap.start()
    swap.wait()

    for tap in range(9):
        for i in range(3):
            rows = []
            for part in range(8):
                first = tap * 192 + i * 64 + part * 8
                rows.append(final[first // 72, pl.ds(first % 72, 8), :].astype(F32))
            gw2_ref[tap // 3, tap % 3, i] = jnp.concatenate(rows, axis=0) * scale_two
        rows = []
        for part in range(8):
            first = 1728 + tap * 64 + part * 8
            rows.append(final[first // 72, pl.ds(first % 72, 8), :].astype(F32))
        s = jnp.concatenate(rows, axis=0)
        turned = jnp.transpose(s)
        for i in range(3):
            gw1_ref[tap // 3, tap % 3, i] = turned[i * 32:i * 32 + 32] * scale_one
        if tap == 0:
            gb1_ref[...] = turned[96:97] * scale_one
        if tap == 1:
            lane_one = lax.broadcasted_iota(jnp.int32, (1, 128), 1)
            out = jnp.zeros((1, 128), F32)
            for quarter in range(4):
                moved = s[quarter:quarter + 1]
                if quarter != 3:
                    moved = pltpu.roll(moved, 32 + 32 * quarter, 1)
                out = jnp.where(lane_one // 32 == quarter, moved, out)
            gb2_ref[...] = out * scale_two


def local(act_in, weight_one, bias_one, weight_two, bias_two, cotangent):
    scale_one = 16.0 / math.sqrt(16 * 32 * 64 * 64)
    scale_two = 1.0 / math.sqrt(16 * 16 * 32 * 32)
    vmem = pl.BlockSpec(memory_space=pltpu.VMEM)
    scratch = [
        pltpu.VMEM((2304, 256), BF16),
        pltpu.VMEM((2304, 256), BF16),
        pltpu.VMEM((17, 80, 128), F32),
        pltpu.VMEM((4, 4, 32, 2176), BF16),
        pltpu.VMEM((2, 64, 2048), BF16),
        pltpu.VMEM((4, 512, 256), F32),
        pltpu.VMEM((48, 2176), F32),
        pltpu.VMEM((32, 2048), BF16),
        pltpu.VMEM((2, 32, 2048), BF16),
        pltpu.VMEM((3, 3, 32, 2176), BF16),
        pltpu.VMEM((3, 512, 256), BF16),
        pltpu.VMEM((2, 32, 2176), BF16),
        pltpu.VMEM((2, 32, 2176), BF16),
        pltpu.VMEM((32, 2176), F32),
        pltpu.VMEM((32, 2048), F32),
        pltpu.VMEM((2, 4, 512, 256), BF16),
        pltpu.VMEM((256, 2048), BF16),
        pltpu.VMEM((2, 2, 32, 2176), BF16),
        pltpu.VMEM((2, 2, 32, 2176), BF16),
        pltpu.VMEM((2, 2, 32, 2176), F32),
        pltpu.VMEM((16, 64, 128), F32),
        pltpu.VMEM((32, 72, 128), F32),
        pltpu.VMEM((16, 72, 128), F32),
        pltpu.VMEM((16, 72, 128), LINK),
        pltpu.VMEM((15, 72, 128), LINK),
        pltpu.VMEM((8, 72, 128), LINK),
        pltpu.VMEM((32, 72, 128), LINK),
        pltpu.SemaphoreType.DMA((4, 2)),
        pltpu.SemaphoreType.DMA((4, 2)),
        pltpu.SemaphoreType.DMA((15,)),
        pltpu.SemaphoreType.DMA((15,)),
        pltpu.SemaphoreType.DMA((7,)),
        pltpu.SemaphoreType.DMA((7,)),
        pltpu.SemaphoreType.DMA((15,)),
        pltpu.SemaphoreType.DMA((15,)),
        pltpu.SemaphoreType.DMA((2,)),
        pltpu.SemaphoreType.DMA((2,)),
    ]
    gx, gw1, gb1, gw2, gb2 = pl.pallas_call(
        functools.partial(kernel, scale_one, scale_two),
        out_shape=(
            jax.ShapeDtypeStruct((1, 2, 64, 2048), BF16),
            jax.ShapeDtypeStruct((3, 3, 3, 32, 64), F32),
            jax.ShapeDtypeStruct((1, 64), F32),
            jax.ShapeDtypeStruct((3, 3, 3, 64, 128), F32),
            jax.ShapeDtypeStruct((1, 128), F32),
        ),
        in_specs=[vmem] * 6,
        out_specs=(vmem,) * 5,
        scratch_shapes=scratch,
        compiler_params=pltpu.CompilerParams(
            collective_id=0, has_side_effects=True, vmem_limit_bytes=60 * 1024 * 1024),
    )(act_in, weight_one, bias_one.reshape(1, 64), weight_two, bias_two.reshape(1, 128), cotangent)
    return gx, gw1, gb1.reshape(64), gw2, gb2.reshape(128)


def solution(mesh):
    placed = (P("dp", "space", None, None), P(), P(), P(), P(), P("dp", "space", None, None))
    return jax.shard_map(
        local,
        mesh=mesh,
        in_specs=placed,
        out_specs=(P("dp", "space", None, None), P(), P(), P(), P()),
        check_vma=False,
    )
```

time: 481 us -> 79.5 us (0.17); the launches traced: 472 us -> 79.4 us
  waiting for transfers between devices: 157 us -> 0 us
  matrix products: 108 us -> 0 us
  blocking collectives: 83 us -> 0 us
  Pallas kernels: 0 us -> 74 us
  local copies, waits for them, and re-layouts: 64.9 us -> 4.7 us
  starting transfers between devices: 25 us -> 0 us
  other arithmetic: 19.1 us -> 0 us
  between operations: 15 us -> 0.66 us
    psum x1 -> x0, waiting for transfers between devices: 144 us -> none  [local(): gw_one, gb_one = lax.psum((gw_one, gb_one), ('dp', 'space'))]
    conv_general_dilated x6 -> x0, matrix products: 108 us -> none  [the longest x2 74.3 us: weight_grad(): lax.conv_general_dilated(padded, delta, (1, 1, 1), ((0, 0), (1, 1), (1, 1...]
    psum x1 -> x0, blocking collectives: 83 us -> none  [local(): gw_one, gb_one = lax.psum((gw_one, gb_one), ('dp', 'space'))]
    pallas_call x0 -> x1, Pallas kernels: none -> 74 us  [local(): pl.pallas_call(functools.partial(kernel, scale_one, scale_two), out_shape...]
    ppermute x8 -> x0, starting transfers between devices: 25 us -> none  [the longest x4 19.2 us: padded_2(): lax.ppermute(tail, axis, [(i, (i + 1) % count) for i in range(ends)])]
    reshape x4 -> x0, local copies, waits for them, and re-layouts: 17.5 us -> none  [the longest x2 15 us: local(): padded_2(act_in, (('space', 1),), 1)]
    conv_general_dilated x9 -> x0, local copies, waits for them, and re-layouts: 15.8 us -> none  [the longest x4 8.76 us: forward_conv(): lax.conv_general_dilated(padded, kernel, (1, 1, 1), ((0, 0), (1, 1), (1,...]
    ppermute x8 -> x0, waiting for transfers between devices: 13.4 us -> none  [the longest x4 9.27 us: padded_2(): lax.ppermute(tail, axis, [(i, (i + 1) % count) for i in range(ends)])]
  transfers between devices with their start and end apart: 9 -> 0, of which waited for: 3 -> 0; matrix products, arithmetic and copies ran while one was open for 29% -> 0% of each run, Pallas kernels for 0% -> 0%
where the time goes in v1:
time: 79.5 us; the launch traced here: 79.4 us
  Pallas kernels  74 us (93%)
  local copies, waits for them, and re-layouts  4.7 us (6%)
    pallas_call x1, Pallas kernels, local(): pl.pallas_call(functools.partial(kernel, scale_one, scale_two), out_shape...  74 us
    unnamed x13, local copies, waits for them, and re-layouts  4.7 us

profile of v1, /device:TPU:1, one launch (start us, length us, event | category | flops | bytes accessed | tf_op | source)
XLA Modules:
  0.0 79.4 jit_solution(14587827408130725286)
XLA Ops:
  0.6 74.0 %shard_map.101 = (bf16[1,2,64,2048]{3,2,1,0:T(8,128)(2,1)}, f32[3,3,3,32,64]{4,3,2,1,0:T(8,128)}, f32[1,64]{1,0:T(1,128)}, f32[3,3,3,64,128]{4,3,2,1,0:T(8,128)}, f32[1,128]{1,0:T(1,128)}) custom-call(bf16[1,2,64,2048]{3,2,1,0:T(8,128)(2,1)} %x_ref.1, bf16[3,3,3,32,64]{4,3,2,1,0:T(8,128)(2,1)} %w1_ref.1, f32[1,64]{1,0:T(1,128)} %bitcast.4, ...), custom_call_target="tpu_custom_call" | custom-call | tf_op jit(solution)/shard_map/pallas_call | solution.py:471
  74.7 0.0 copy-start.1
  74.7 0.0 copy-start
  74.7 2.0 %copy.16 = bf16[1,2,64,2048]{3,2,1,0:T(8,128)(2,1)} copy(bf16[1,2,64,2048]{3,2,1,0:T(8,128)(2,1)} %get-tuple-element.20) | data formatting | bytes 1048576
  76.7 0.0 copy-done.1
  76.7 0.0 copy-start.3
  76.7 0.8 copy.17
  77.4 0.0 copy-done.3
  77.4 0.5 copy.18
  78.0 0.0 copy-done
  78.0 0.0 copy-start.2
  78.0 0.9 %copy.19 = f32[3,3,3,64,128]{4,3,2,1,0:T(8,128)} copy(f32[3,3,3,64,128]{4,3,2,1,0:T(8,128)S(1)} %copy-done) | data formatting | bytes 1769472
  78.9 0.0 copy-done.2
  78.9 0.5 copy.20
Async XLA Ops:
  74.7 2.0 %copy-start.1 = (f32[3,3,3,32,64]{4,3,2,1,0:T(8,128)S(1)}, f32[3,3,3,32,64]{4,3,2,1,0:T(8,128)}, u32[]{:S(2)}) copy-start(f32[3,3,3,32,64]{4,3,2,1,0:T(8,128)} %get-tuple-element.21) | copy-start | bytes 663556
  74.7 3.3 %copy-start = (f32[3,3,3,64,128]{4,3,2,1,0:T(8,128)S(1)}, f32[3,3,3,64,128]{4,3,2,1,0:T(8,128)}, u32[]{:S(2)}) copy-start(f32[3,3,3,64,128]{4,3,2,1,0:T(8,128)} %get-tuple-element.23) | copy-start | bytes 2654212
  76.7 0.8 copy-start.3
  78.0 0.9 %copy-start.2 = (f32[1,128]{1,0:T(1,128)S(1)}, f32[1,128]{1,0:T(1,128)}, u32[]{:S(2)}) copy-start(f32[1,128]{1,0:T(1,128)} %get-tuple-element.14) | copy-start | bytes 1540

commit v2 on v0

v2 whole, which is shorter than its diff:
```python
import functools
import math

import jax
import jax.numpy as jnp
from jax import lax
from jax.experimental import pallas as pl
from jax.experimental.pallas import tpu as pltpu
from jax.sharding import PartitionSpec as P

F32 = jnp.float32
BF16 = jnp.bfloat16
LINK1 = jnp.bfloat16
LINK2 = jnp.bfloat16
MESH = pl.DeviceIdType.MESH

E0, O0, EP, OM = 0, 1, 2, 3
FWD = ((OM, E0, O0), (E0, O0, EP))
BWD = ((O0, E0, OM), (EP, O0, E0))

NT = (((1,), (1,)), ((), ()))
TN = (((0,), (0,)), ((), ()))

X_CUT = (0, 9, 16)
ROWS2 = 56
ROWS1 = 16


def dot(a, b):
    return jnp.dot(a, b, preferred_element_type=F32)


def slope_of(value, sig):
    return sig * (1.0 + value * (1.0 - sig))


def sigmoid(value):
    return 0.5 * jnp.tanh(0.5 * value) + 0.5


def kernel(
    x_hbm, w1_hbm, b1_hbm, w2_hbm, b2_hbm, cot_hbm,
    gx_buf, fin1, fin2,
    x_a, x_b, w1_ref, b1_ref, w2_ref, b2_ref, cot_ref,
    t1, t2, xf, xv, halo_a, halo_b, slope, pf, pool, halo_p, ps, pre_two, d2, gs_a, gs_b, gr_a, gr_b, gown,
    d1, d1t, xsend, xrecv, xown, outf,
    acc1, half1, r11, r21,
    acc2, r02, half2, r12, r22,
    l_sem, s_send, s_recv, a_send, a_recv, z_send, z_recv, g_send, g_recv, c_send, c_recv, b_send, b_recv,
):
    dp = lax.axis_index("dp")
    space = lax.axis_index("space")
    nxt = lax.rem(space + 1, 16)
    prv = lax.rem(space + 15, 16)
    core = lax.rem(dp, 2)
    x_pos = lax.rem(dp // 2, 2) * 2 + space // 8
    chip = (dp // 4) * 4 + x_pos
    z = lax.rem(space, 8)
    partner = (dp + 1 - 2 * core, space)

    def chip_at(r):
        q = lax.rem(chip + r, 16)
        qx = lax.rem(q, 4)
        return (q // 4) * 4 + (qx // 2) * 2 + core, lax.rem(qx, 2) * 8 + z, q

    def other_at(r):
        da, db, q = chip_at(r)
        return da + 1 - 2 * core, db, q

    def z_at(r):
        return dp, (space // 8) * 8 + lax.rem(z + r, 8)

    barrier = pltpu.get_barrier_semaphore()

    def greet(device):
        pl.semaphore_signal(barrier, inc=1, device_id=device, device_id_type=MESH)

    loads = []
    for i, (src, dst) in enumerate((
        (x_hbm.at[0, :, :, pl.ds(0, 1152)], x_a), (x_hbm.at[0, :, :, pl.ds(1152, 896)], x_b),
        (w1_hbm, w1_ref), (w2_hbm, w2_ref), (b1_hbm, b1_ref), (b2_hbm, b2_ref), (cot_hbm, cot_ref),
    )):
        cp = pltpu.make_async_copy(src, dst, l_sem.at[i])
        cp.start()
        loads.append(cp)

    greet((dp, nxt))
    greet((dp, prv))
    for r in range(1, 8):
        greet(z_at(r))
    for r in range(1, 16):
        greet(chip_at(r)[:2])
    for r in range(16):
        greet(other_at(r)[:2])

    not_last = space < 15
    not_first = space > 0

    def exchange(down, up, from_next, from_prev, stage):
        one = pltpu.make_async_remote_copy(
            src_ref=down, dst_ref=from_next, send_sem=s_send.at[stage, 0], recv_sem=s_recv.at[stage, 0],
            device_id=(dp, prv), device_id_type=MESH)
        two = pltpu.make_async_remote_copy(
            src_ref=up, dst_ref=from_prev, send_sem=s_send.at[stage, 1], recv_sem=s_recv.at[stage, 1],
            device_id=(dp, nxt), device_id_type=MESH)

        @pl.when(not_first)
        def _():
            one.start()

        @pl.when(not_last)
        def _():
            two.start()
        return one, two

    def finish(pair):
        one, two = pair

        @pl.when(not_first)
        def _():
            one.wait_send()
            two.wait_recv()

        @pl.when(not_last)
        def _():
            two.wait_send()
            one.wait_recv()

    loads[0].wait()
    loads[1].wait()
    pl.semaphore_wait(barrier, 40)
    x_pairs = [
        exchange(x_a.at[0], x_a.at[1], halo_a.at[1], halo_a.at[0], 0),
        exchange(x_b.at[0], x_b.at[1], halo_b.at[1], halo_b.at[0], 1),
    ]

    @pl.when(jnp.logical_not(not_first))
    def _():
        halo_a[0] = jnp.zeros(halo_a.shape[1:], BF16)
        halo_b[0] = jnp.zeros(halo_b.shape[1:], BF16)
        halo_p[0] = jnp.zeros(halo_p.shape[1:], BF16)
        gr_a[0] = jnp.zeros(gr_a.shape[1:], BF16)
        gr_b[0] = jnp.zeros(gr_b.shape[1:], BF16)
        xrecv[0] = jnp.zeros(xrecv.shape[1:], BF16)

    @pl.when(jnp.logical_not(not_last))
    def _():
        halo_a[1] = jnp.zeros(halo_a.shape[1:], BF16)
        halo_b[1] = jnp.zeros(halo_b.shape[1:], BF16)
        halo_p[1] = jnp.zeros(halo_p.shape[1:], BF16)
        gr_a[1] = jnp.zeros(gr_a.shape[1:], BF16)
        gr_b[1] = jnp.zeros(gr_b.shape[1:], BF16)
        xrecv[1] = jnp.zeros(xrecv.shape[1:], BF16)

    lane = lax.broadcasted_iota(jnp.int32, (64, 128), 1)

    def prepare(src, side, plane, first, last):
        def turned(t):
            if t < 0 or t > 15:
                return jnp.zeros((64, 128), F32)
            c = 0 if t < X_CUT[1] else 1
            v = src[c][side, :, (t - X_CUT[c]) * 128:(t - X_CUT[c]) * 128 + 128].astype(F32)
            return pltpu.roll(v, 32, 1)
        before = turned(first - 1)
        for t in range(first, last):
            here = turned(t)
            xf[t, 8:72, :] = jnp.where(lane < 32, before, here)
            before = here
            at = pl.ds(t * 128, 128)
            xv[plane, E0, :, at] = xf[t, pl.ds(8, 32, stride=2), :].astype(BF16)
            xv[plane, O0, :, at] = xf[t, pl.ds(9, 32, stride=2), :].astype(BF16)
            xv[plane, EP, :, at] = xf[t, pl.ds(10, 32, stride=2), :].astype(BF16)
            xv[plane, OM, :, at] = xf[t, pl.ds(7, 32, stride=2), :].astype(BF16)

    xf[:, 0:8, :] = jnp.zeros((17, 8, 128), F32)
    xf[:, 72:80, :] = jnp.zeros((17, 8, 128), F32)
    pf[0:8, :] = jnp.zeros((8, 2176), F32)
    pf[40:48, :] = jnp.zeros((8, 2176), F32)

    loads[2].wait()
    for k in range(3):
        for j in range(3):
            w = w1_ref[k, j].reshape(96, 64).astype(F32)
            for t in range(2):
                cols = []
                for v in (t, t + 2):
                    parts = [w]
                    if v:
                        parts = [jnp.zeros((32 * v, 64), F32)] + parts
                    parts = parts + [jnp.zeros((160 - 32 * v, 64), F32)]
                    cols.append(jnp.concatenate(parts, axis=0))
                t1[pl.ds((k * 3 + j) * 256, 256), pl.ds(t * 128, 128)] = jnp.concatenate(cols, axis=1).astype(BF16)

    prepare((x_a, x_b), 0, 1, 0, 17)
    prepare((x_a, x_b), 1, 2, 0, 17)

    for i in range(3, 7):
        loads[i].wait()
    for k in range(3):
        for j in range(3):
            w = w2_ref[k, j].reshape(192, 128)
            gap = jnp.zeros((64, 128), BF16)
            t2[pl.ds((k * 3 + j) * 256, 256), pl.ds(0, 128)] = jnp.concatenate([w, gap], axis=0)
            t2[pl.ds((k * 3 + j) * 256, 256), pl.ds(128, 128)] = jnp.concatenate([gap, w], axis=0)

    bias = jnp.concatenate([b1_ref[...], b1_ref[...]], axis=1)
    bias = jnp.concatenate([bias, bias], axis=1)

    def lhs_one(d, ks, first, blocks):
        return jnp.concatenate([
            jnp.concatenate([
                xv[d + k, FWD[p][j], :, pl.ds(pl.multiple_of((first + b) * 128, 128), 256)]
                for p in range(2) for b in range(blocks)], axis=0)
            for k in ks for j in range(3)], axis=1)

    def own_one(g, carry):
        for d in range(2):
            part = dot(lhs_one(d, (1 - d, 2 - d), g * 8, 8), t1[pl.ds((1 - d) * 768, 1536), :])
            for p in range(2):
                slope[d * 2 + p, pl.ds(pl.multiple_of(g * 256, 256), 256), :] = part[p * 256:p * 256 + 256]
        return carry
    lax.fori_loop(0, 2, own_one, 0)

    p_pairs = []
    for g in range(2):
        finish(x_pairs[g])
        prepare((halo_a, halo_b), 0, 0, (0, 9)[g], (9, 17)[g])
        prepare((halo_a, halo_b), 1, 3, (0, 9)[g], (9, 17)[g])
        sums = [None] * 8
        rows = pl.ds(g * 256, 256)
        for d in range(2):
            part = dot(lhs_one(d, (2 * d,), g * 8, 8), t1[pl.ds(2 * d * 768, 768), :])
            for p in range(2):
                pre = part[p * 256:p * 256 + 256] + slope[d * 2 + p, rows, :] + bias
                sig = sigmoid(pre)
                act = pre * sig
                slope[d * 2 + p, rows, :] = slope_of(pre, sig) * 0.125
                for b in range(8):
                    piece = act[b * 32:b * 32 + 32, 0:128] + act[b * 32:b * 32 + 32, 128:256]
                    sums[b] = piece if sums[b] is None else sums[b] + piece
        for b in range(8):
            pool[g, :, b * 128:b * 128 + 128] = (sums[b] * 0.125).astype(BF16)
        p_pairs.append(exchange(pool.at[g], pool.at[g], halo_p.at[1, g], halo_p.at[0, g], 2 + g))

    lane_p = lax.broadcasted_iota(jnp.int32, (32, 128), 1)

    def prepare_pool(src, plane, first, last):
        def turned(t):
            if t < 0 or t > 15:
                return jnp.zeros((32, 128), F32)
            v = src[t // 8, :, t % 8 * 128:t % 8 * 128 + 128].astype(F32)
            return pltpu.roll(v, 64, 1)
        before = turned(first - 1)
        for t in range(first, last):
            here = turned(t)
            at = pl.ds(t * 128, 128)
            pf[8:40, at] = jnp.where(lane_p < 64, before, here)
            before = here
            for j in range(3):
                ps[plane, j, :, at] = pf[7 + j:39 + j, at].astype(BF16)

    def lhs_two(ks, first, blocks):
        return jnp.concatenate([
            jnp.concatenate([ps[k, j, :, pl.ds((first + b) * 128, 256)] for b in range(blocks)], axis=0)
            for k in ks for j in range(3)], axis=1)

    prepare_pool(pool, 1, 0, 17)
    pre_two[...] = dot(lhs_two((1,), 0, 16), t2[pl.ds(768, 768), :])

    row = lax.broadcasted_iota(jnp.int32, (32, 256), 0)
    bias_two = jnp.concatenate([b2_ref[...], b2_ref[...]], axis=1)

    def shift_up(v):
        return jnp.where(row < 31, pltpu.roll(v, 31, 0), 0.0)

    def shift_down(v):
        return jnp.where(row > 0, pltpu.roll(v, 1, 0), 0.0)

    def window_tiles(win, base, carried, put):
        blocks = win.shape[0] // 32
        for t in range(blocks):
            piece = win[t * 32:t * 32 + 32, 0:128]
            if carried is not None:
                piece = piece + carried
            put(base + t, piece)
            carried = win[t * 32:t * 32 + 32, 128:256]
        return carried

    total_two = jnp.zeros((32, 256), F32)
    g_pairs = []
    carried = [None, None, None]
    done = 0
    for half in range(2):
        if half == 0:
            finish(p_pairs[0])
            finish(p_pairs[1])
        upto = (9, 17)[half]
        prepare_pool(halo_p.at[0], 0, done, upto)
        prepare_pool(halo_p.at[1], 2, done, upto)
        done = upto
        pre = pre_two[pl.ds(half * 256, 256), :] + bias_two
        pre = pre + dot(lhs_two((0, 2), half * 8, 8), jnp.concatenate([t2[0:768, :], t2[1536:2304, :]], axis=0))
        slp = slope_of(pre, sigmoid(pre))
        for b in range(8):
            block = half * 8 + b
            rows = pl.ds(block * 32, 32)
            delta = (cot_ref[0, 0, :, block * 256:block * 256 + 256].astype(F32) * slp[b * 32:b * 32 + 32]).astype(BF16)
            wide = delta.astype(F32)
            d2[1, rows, :] = delta
            d2[0, rows, :] = shift_up(wide).astype(BF16)
            d2[2, rows, :] = shift_down(wide).astype(BF16)
            total_two = total_two + wide
        rows = pl.ds(half * 256, 256)
        lhs = jnp.concatenate([d2[0, rows, :], d2[1, rows, :], d2[2, rows, :]], axis=1)
        for k in (0, 2):
            rhs = jnp.concatenate([t2[pl.ds((k * 3 + j) * 256, 256), :] for j in range(3)], axis=1)
            win = lax.dot_general(lhs, rhs, NT, preferred_element_type=F32)

            def put(t, piece, k=k):
                ref, t = (gs_a, t) if t < 8 else (gs_b, t - 8)
                ref[k // 2, :, t * 128:t * 128 + 128] = piece.astype(BF16)
            carried[k] = window_tiles(win, half * 8, carried[k], put)
            if half == 1:
                put(16, carried[k])
        put, got = ((gs_a, gr_a), (gs_b, gr_b))[half]
        g_pairs.append(exchange(put.at[0], put.at[1], got.at[1], got.at[0], 4 + half))

    two = jnp.sum(total_two, axis=0, keepdims=True)
    acc2[216 // 7, pl.ds((216 % 7) * 8, 8), :] = jnp.broadcast_to(two[:, 0:128] + two[:, 128:256], (8, 128))
    for unit in range(217, 224):
        acc2[unit // 7, pl.ds((unit % 7) * 8, 8), :] = jnp.zeros((8, 128), F32)
    for k in range(3):
        for j in range(3):
            lhs = jnp.concatenate([ps[k, j, :, b * 128:b * 128 + 256] for b in range(16)], axis=0)
            g = lax.dot_general(lhs, d2[1], TN, preferred_element_type=F32)
            s = g[0:192, 0:128] + g[64:256, 128:256]
            for part in range(24):
                unit = (k * 3 + j) * 24 + part
                acc2[unit // 7, pl.ds((unit % 7) * 8, 8), :] = s[part * 8:part * 8 + 8]

    def swap_start(a, acc, r0):
        cp = pltpu.make_async_remote_copy(
            src_ref=acc.at[pl.ds((1 - core) * 16, 16)], dst_ref=r0, send_sem=c_send.at[a, 0], recv_sem=c_recv.at[a, 0],
            device_id=partner, device_id_type=MESH)
        cp.start()
        return cp

    def plane_start(a, swap, acc, r0, half, r1):
        swap.wait()

        def add_half(i, carry):
            half[i] = (acc[core * 16 + i] + r0[i]).astype(half.dtype)
            return carry
        lax.fori_loop(0, 16, add_half, 0)
        sends = []
        for r in range(1, 16):
            da, db, q = chip_at(r)
            cp = pltpu.make_async_remote_copy(
                src_ref=half.at[q], dst_ref=r1.at[r - 1], send_sem=a_send.at[a, r - 1], recv_sem=a_recv.at[a, r - 1],
                device_id=(da, db), device_id_type=MESH)
            cp.start()
            sends.append(cp)
        return sends

    def column_start(a, sends, half, r1, r2):
        piece = half[chip + (core * 16 if a == 0 else 0)].astype(F32)
        for r in range(len(sends)):
            sends[r].wait()
            piece = piece + r1[r].astype(F32)
        r2[z] = piece.astype(r2.dtype)
        sends = []
        for r in range(1, 8):
            cp = pltpu.make_async_remote_copy(
                src_ref=r2.at[z], dst_ref=r2.at[z], send_sem=z_send.at[a, r - 1], recv_sem=z_recv.at[a, r - 1],
                device_id=z_at(r), device_id_type=MESH)
            cp.start()
            sends.append(cp)
        return sends

    def gather_start(a, sends, r2, final):
        for cp in sends:
            cp.wait()
        piece = r2[0].astype(F32)
        for i in range(1, 8):
            piece = piece + r2[i].astype(F32)
        mine = core * 16 + chip
        final[mine] = piece.astype(final.dtype)
        sends = []
        for r in range(1, 16):
            da, db, q = chip_at(r)
            cp = pltpu.make_async_remote_copy(
                src_ref=final.at[mine], dst_ref=final.at[mine], send_sem=g_send.at[a, r - 1], recv_sem=g_recv.at[a, r - 1],
                device_id=(da, db), device_id_type=MESH)
            cp.start()
            sends.append(cp)
        return sends

    def back_start(a, sends, final):
        for cp in sends:
            cp.wait()
        cp = pltpu.make_async_remote_copy(
            src_ref=final.at[pl.ds(core * 16, 16)], dst_ref=final.at[pl.ds(core * 16, 16)],
            send_sem=c_send.at[a, 1], recv_sem=c_recv.at[a, 1], device_id=partner, device_id_type=MESH)
        cp.start()
        return cp

    def scatter_start():
        def convert(i, carry):
            half1[i] = acc1[i].astype(half1.dtype)
            return carry
        lax.fori_loop(0, 32, convert, 0)
        sends = []
        for r in range(31):
            da, db, q = chip_at(r + 1) if r < 15 else other_at(r - 15)
            owner = (core if r < 15 else 1 - core) * 16 + q
            cp = pltpu.make_async_remote_copy(
                src_ref=half1.at[owner], dst_ref=r11.at[r], send_sem=b_send.at[0, r], recv_sem=b_recv.at[0, r],
                device_id=(da, db), device_id_type=MESH)
            cp.start()
            sends.append(cp)
        return sends

    def spread_start(sends):
        for cp in sends:
            cp.wait()
        piece = r21[0].astype(F32)
        for i in range(1, 8):
            piece = piece + r21[i].astype(F32)
        mine = core * 16 + chip
        fin1[mine] = piece.astype(fin1.dtype)
        sends = []
        for r in range(31):
            da, db, q = chip_at(r + 1) if r < 15 else other_at(r - 15)
            cp = pltpu.make_async_remote_copy(
                src_ref=fin1.at[mine], dst_ref=fin1.at[mine], send_sem=b_send.at[1, r], recv_sem=b_recv.at[1, r],
                device_id=(da, db), device_id_type=MESH)
            cp.start()
            sends.append(cp)
        return sends

    run2 = swap_start(1, acc2, r02)

    lhs = jnp.concatenate([d2[0], d2[1], d2[2]], axis=1)
    rhs = jnp.concatenate([t2[pl.ds((3 + j) * 256, 256), :] for j in range(3)], axis=1)

    def put_own(t, piece):
        gown[:, t * 128:t * 128 + 128] = piece
    put_own(16, window_tiles(lax.dot_general(lhs, rhs, NT, preferred_element_type=F32), 0, None, put_own))

    def pooled_tile(t, got, base):
        at = pl.ds(pl.multiple_of(t * 128, 128), 128)
        there = pl.ds(pl.multiple_of((t - base) * 128, 128), 128)
        v = gown[:, at] + got[0, :, there].astype(F32) + got[1, :, there].astype(F32)
        return pltpu.roll(v, 64, 1)

    def delta_one(got, base, b, carry):
        total, before = carry
        after = pooled_tile(b + 1, got, base)
        g = jnp.where(lane_p < 64, before, after)
        g = jnp.concatenate([g, g], axis=1)
        rows = pl.ds(pl.multiple_of(b * 32, 32), 32)
        for d in range(2):
            for p in range(2):
                delta = (g * slope[d * 2 + p, rows, :]).astype(BF16)
                wide = delta.astype(F32)
                d1[d, E0 if p == 0 else O0, rows, :] = delta
                if p == 0:
                    d1[d, EP, rows, :] = shift_up(wide).astype(BF16)
                else:
                    d1[d, OM, rows, :] = shift_down(wide).astype(BF16)
                total = total + wide
        return total, after

    finish(g_pairs[0])
    carry = lax.fori_loop(
        0, 7, functools.partial(delta_one, gr_a, 0), (jnp.zeros((32, 256), F32), pooled_tile(0, gr_a, 0)))
    finish(g_pairs[1])
    run2 = plane_start(1, run2, acc2, r02, half2, r12)
    total_one, _ = lax.fori_loop(7, 16, functools.partial(delta_one, gr_b, 8), carry)

    def window_one(terms, q):
        lhs = jnp.concatenate([d1[d, BWD[q][j]] for d, k in terms for j in range(3)], axis=1)
        rhs = jnp.concatenate([t1[pl.ds((k * 3 + j) * 256, 256), :] for d, k in terms for j in range(3)], axis=1)
        return lax.dot_general(lhs, rhs, NT, preferred_element_type=F32)

    x_pairs = []
    for q in range(2):
        for side, terms in ((0, ((0, 0),)), (1, ((1, 2),))):
            def put(t, piece, side=side, q=q):
                xsend[side, q, :, t * 128:t * 128 + 128] = piece.astype(BF16)
            put(16, window_tiles(window_one(terms, q), 0, None, put))
        x_pairs.append(exchange(xsend.at[0, q], xsend.at[1, q], xrecv.at[1, q], xrecv.at[0, q], 6 + q))
    for d in range(2):
        for p in range(2):
            for c in range(4):
                v = d1[d, p, pl.ds(c * 128, 128), :]
                d1t[:, pl.ds((d * 2 + p) * 512 + c * 128, 128)] = jnp.transpose(v)

    total = jnp.sum(total_one, axis=0, keepdims=True)
    total = total[:, 0:128] + total[:, 128:256]
    total = total + pltpu.roll(total, 64, 1)
    total_col = jnp.sum(
        jnp.where(lane == lax.broadcasted_iota(jnp.int32, (64, 128), 0), total, 0.0), axis=1, keepdims=True)

    def tap_one(tap):
        k, j = tap // 3, tap % 3
        rhs = jnp.concatenate([
            xv[d + k, FWD[p][j], :, b * 128:b * 128 + 256]
            for d in range(2) for p in range(2) for b in range(16)], axis=0)
        g = dot(d1t[...], rhs)
        s = g[0:64, 0:128] + pltpu.roll(g[128:192, 0:128], 128 - 32, 1)
        s = s + pltpu.roll(g[64:128, 0:256], 256 - 64, 1)[:, 0:128]
        return s + pltpu.roll(g[192:256, 0:256], 256 - 96, 1)[:, 0:128]

    last = tap_one(8)
    for tap in range(8):
        s = tap_one(tap)
        extra = pltpu.roll(last, 96 - 32 * tap, 1) if tap < 3 else total_col
        s = jnp.where(lane < 96, s, extra)
        for part in range(8):
            unit = tap * 8 + part
            acc1[unit // 2, pl.ds((unit % 2) * 8, 8), :] = s[part * 8:part * 8 + 8]
    run1 = scatter_start()

    run2 = column_start(1, run2, half2, r12, r22)

    def own_planes(e, terms):
        for q in range(2):
            def put(t, piece, q=q):
                xown[e, q, :, t * 128:t * 128 + 128] = piece
            put(16, window_tiles(window_one(terms, q), 0, None, put))
    own_planes(0, ((0, 1), (1, 0)))
    own_planes(1, ((0, 2), (1, 1)))
    run1 = column_start(0, run1, half1, r11, r21)
    run2 = gather_start(1, run2, r22, fin2)
    run1 = spread_start(run1)
    run2 = back_start(1, run2, fin2)

    for q in range(2):
        finish(x_pairs[q])
        for e in range(2):
            def tile(t):
                at = pl.ds(t * 128, 128)
                v = xown[e, q, :, at]
                v = v + xrecv[e, q, :, at].astype(F32)
                return pltpu.roll(v, 96, 1)
            before = tile(0)
            for t in range(16):
                after = tile(t + 1)
                outf[e, t, pl.ds(q, 32, stride=2), :] = jnp.where(lane_p < 96, before, after)
                before = after
    for e in range(2):
        for t in range(16):
            gx_buf[0, e, :, t * 128:t * 128 + 128] = outf[e, t].astype(BF16)

    run2.wait()
    for cp in run1:
        cp.wait()


def unpack(scale_one, scale_two, gx_in, final1, final2, gx_ref, gw1_ref, gb1_ref, gw2_ref, gb2_ref):
    gx_ref[...] = gx_in[...]

    def unit_two(unit):
        return final2[unit // 7, pl.ds((unit % 7) * 8, 8), :].astype(F32)

    for tap in range(9):
        for i in range(3):
            for part in range(8):
                gw2_ref[tap // 3, tap % 3, i, pl.ds(part * 8, 8), :] = unit_two(tap * 24 + i * 8 + part) * scale_two
    gb2_ref[...] = unit_two(216)[0:1] * scale_two
    for tap in range(8):
        turned = jnp.transpose(final1[pl.ds(tap * 4, 4)].reshape(64, 128).astype(F32)) * scale_one
        for i in range(3):
            gw1_ref[tap // 3, tap % 3, i] = turned[i * 32:i * 32 + 32]
        if tap < 3:
            gw1_ref[2, 2, tap] = turned[96:128]
        if tap == 3:
            gb1_ref[...] = turned[96:97]


def local(act_in, weight_one, bias_one, weight_two, bias_two, cotangent):
    scale_one = 16.0 / math.sqrt(16 * 32 * 64 * 64)
    scale_two = 1.0 / math.sqrt(16 * 16 * 32 * 32)
    vmem = pl.BlockSpec(memory_space=pltpu.VMEM)
    anywhere = pl.BlockSpec(memory_space=pltpu.HBM)
    scratch = [
        pltpu.VMEM((2, 64, 1152), BF16),
        pltpu.VMEM((2, 64, 896), BF16),
        pltpu.VMEM((3, 3, 3, 32, 64), BF16),
        pltpu.VMEM((1, 64), F32),
        pltpu.VMEM((3, 3, 3, 64, 128), BF16),
        pltpu.VMEM((1, 128), F32),
        pltpu.VMEM((1, 1, 32, 4096), BF16),
        pltpu.VMEM((2304, 256), BF16),
        pltpu.VMEM((2304, 256), BF16),
        pltpu.VMEM((17, 80, 128), F32),
        pltpu.VMEM((4, 4, 32, 2176), BF16),
        pltpu.VMEM((2, 64, 1152), BF16),
        pltpu.VMEM((2, 64, 896), BF16),
        pltpu.VMEM((4, 512, 256), F32),
        pltpu.VMEM((48, 2176), F32),
        pltpu.VMEM((2, 32, 1024), BF16),
        pltpu.VMEM((2, 2, 32, 1024), BF16),
        pltpu.VMEM((3, 3, 32, 2176), BF16),
        pltpu.VMEM((512, 256), F32),
        pltpu.VMEM((3, 512, 256), BF16),
        pltpu.VMEM((2, 32, 1024), BF16),
        pltpu.VMEM((2, 32, 1152), BF16),
        pltpu.VMEM((2, 32, 1024), BF16),
        pltpu.VMEM((2, 32, 1152), BF16),
        pltpu.VMEM((32, 2176), F32),
        pltpu.VMEM((2, 4, 512, 256), BF16),
        pltpu.VMEM((256, 2048), BF16),
        pltpu.VMEM((2, 2, 32, 2176), BF16),
        pltpu.VMEM((2, 2, 32, 2176), BF16),
        pltpu.VMEM((2, 2, 32, 2176), F32),
        pltpu.VMEM((2, 16, 64, 128), F32),
        pltpu.VMEM((32, ROWS1, 128), F32),
        pltpu.VMEM((32, ROWS1, 128), LINK1),
        pltpu.VMEM((31, ROWS1, 128), LINK1),
        pltpu.VMEM((8, ROWS1, 128), LINK1),
        pltpu.VMEM((32, ROWS2, 128), F32),
        pltpu.VMEM((16, ROWS2, 128), F32),
        pltpu.VMEM((16, ROWS2, 128), LINK2),
        pltpu.VMEM((15, ROWS2, 128), LINK2),
        pltpu.VMEM((8, ROWS2, 128), LINK2),
        pltpu.SemaphoreType.DMA((7,)),
        pltpu.SemaphoreType.DMA((8, 2)),
        pltpu.SemaphoreType.DMA((8, 2)),
        pltpu.SemaphoreType.DMA((2, 15)),
        pltpu.SemaphoreType.DMA((2, 15)),
        pltpu.SemaphoreType.DMA((2, 7)),
        pltpu.SemaphoreType.DMA((2, 7)),
        pltpu.SemaphoreType.DMA((2, 15)),
        pltpu.SemaphoreType.DMA((2, 15)),
        pltpu.SemaphoreType.DMA((2, 2)),
        pltpu.SemaphoreType.DMA((2, 2)),
        pltpu.SemaphoreType.DMA((2, 31)),
        pltpu.SemaphoreType.DMA((2, 31)),
    ]
    gx, final1, final2 = pl.pallas_call(
        kernel,
        out_shape=(
            jax.ShapeDtypeStruct((1, 2, 64, 2048), BF16),
            jax.ShapeDtypeStruct((32, ROWS1, 128), LINK1),
            jax.ShapeDtypeStruct((32, ROWS2, 128), LINK2),
        ),
        in_specs=[anywhere] * 6,
        out_specs=(vmem,) * 3,
        scratch_shapes=scratch,
        compiler_params=pltpu.CompilerParams(
            collective_id=0, has_side_effects=True, vmem_limit_bytes=32 * 1024 * 1024),
    )(*(pltpu.with_memory_space_constraint(v, pltpu.HBM) for v in (
        act_in, weight_one, bias_one.reshape(1, 64), weight_two, bias_two.reshape(1, 128), cotangent)))
    gx, gw1, gb1, gw2, gb2 = pl.pallas_call(
        functools.partial(unpack, scale_one, scale_two),
        out_shape=(
            jax.ShapeDtypeStruct((1, 2, 64, 2048), BF16),
            jax.ShapeDtypeStruct((3, 3, 3, 32, 64), F32),
            jax.ShapeDtypeStruct((1, 64), F32),
            jax.ShapeDtypeStruct((3, 3, 3, 64, 128), F32),
            jax.ShapeDtypeStruct((1, 128), F32),
        ),
        in_specs=[vmem] * 3,
        out_specs=(vmem,) * 5,
        compiler_params=pltpu.CompilerParams(vmem_limit_bytes=16 * 1024 * 1024),
    )(gx, final1, final2)
    return gx, gw1, gb1.reshape(64), gw2, gb2.reshape(128)


def solution(mesh):
    placed = (P("dp", "space", None, None), P(), P(), P(), P(), P("dp", "space", None, None))
    return jax.shard_map(
        local,
        mesh=mesh,
        in_specs=placed,
        out_specs=(P("dp", "space", None, None), P(), P(), P(), P()),
        check_vma=False,
    )
```

time: 481 us -> 56.1 us (0.12); the launches traced: 472 us -> 56 us
  waiting for transfers between devices: 157 us -> 0 us
  matrix products: 108 us -> 0 us
  blocking collectives: 83 us -> 0 us
  local copies, waits for them, and re-layouts: 64.9 us -> 0 us
  Pallas kernels: 0 us -> 55.4 us
  starting transfers between devices: 25 us -> 0 us
  other arithmetic: 19.1 us -> 0 us
  between operations: 15 us -> 0.64 us
    psum x1 -> x0, waiting for transfers between devices: 144 us -> none  [local(): gw_one, gb_one = lax.psum((gw_one, gb_one), ('dp', 'space'))]
    conv_general_dilated x6 -> x0, matrix products: 108 us -> none  [the longest x2 74.3 us: weight_grad(): lax.conv_general_dilated(padded, delta, (1, 1, 1), ((0, 0), (1, 1), (1, 1...]
    psum x1 -> x0, blocking collectives: 83 us -> none  [local(): gw_one, gb_one = lax.psum((gw_one, gb_one), ('dp', 'space'))]
    pallas_call x0 -> x2, Pallas kernels: none -> 55.4 us  [the longest x1 54 us: local(): pl.pallas_call(kernel, out_shape=(jax.ShapeDtypeStruct((1, 2, 64, 2048),...]
    ppermute x8 -> x0, starting transfers between devices: 25 us -> none  [the longest x4 19.2 us: padded_2(): lax.ppermute(tail, axis, [(i, (i + 1) % count) for i in range(ends)])]
    reshape x4 -> x0, local copies, waits for them, and re-layouts: 17.5 us -> none  [the longest x2 15 us: local(): padded_2(act_in, (('space', 1),), 1)]
    conv_general_dilated x9 -> x0, local copies, waits for them, and re-layouts: 15.8 us -> none  [the longest x4 8.76 us: forward_conv(): lax.conv_general_dilated(padded, kernel, (1, 1, 1), ((0, 0), (1, 1), (1,...]
    ppermute x8 -> x0, waiting for transfers between devices: 13.4 us -> none  [the longest x4 9.27 us: padded_2(): lax.ppermute(tail, axis, [(i, (i + 1) % count) for i in range(ends)])]
  transfers between devices with their start and end apart: 9 -> 0, of which waited for: 3 -> 0; matrix products, arithmetic and copies ran while one was open for 29% -> 0% of each run, Pallas kernels for 0% -> 0%
where the time goes in v2:
time: 56.1 us; the launch traced here: 56 us
  Pallas kernels  55.4 us (99%)
  between operations  0.64 us (1%)
    pallas_call x1, Pallas kernels, local(): pl.pallas_call(kernel, out_shape=(jax.ShapeDtypeStruct((1, 2, 64, 2048),...  54 us
    pallas_call x1, Pallas kernels, local(): pl.pallas_call(functools.partial(unpack, scale_one, scale_two), out_shape...  1.41 us

profile of v2, /device:TPU:1, one launch (start us, length us, event | category | flops | bytes accessed | tf_op | source)
XLA Modules:
  0.0 56.0 jit_solution(13993448193778427216)
XLA Ops:
  0.6 54.0 %shard_map.101 = (bf16[1,2,64,2048]{3,2,1,0:T(8,128)(2,1)S(1)}, bf16[32,16,128]{2,1,0:T(8,128)(2,1)S(1)}, bf16[32,56,128]{2,1,0:T(8,128)(2,1)S(1)}) custom-call(bf16[1,2,64,2048]{3,2,1,0:T(8,128)(2,1)} %x_hbm.1, bf16[3,3,3,32,64]{4,3,2,1,0:T(8,128)(2,1)} %w1_hbm.1, f32[1,64]{1,0:T(1,128)} %bitcast.4, bf16[3,3,3,64,128]{4,3,2,1,0:T(8,128)(2,1)} %w2_hbm.1, ...), custom_call_target="tpu_custom_call" | custom-call | tf_op jit(solution)/shard_map/pallas_call | solution.py:642
  54.6 1.4 %shard_map.102 = (bf16[1,2,64,2048]{3,2,1,0:T(8,128)(2,1)}, f32[3,3,3,32,64]{4,3,2,1,0:T(8,128)}, f32[1,64]{1,0:T(1,128)}, f32[3,3,3,64,128]{4,3,2,1,0:T(8,128)}, f32[1,128]{1,0:T(1,128)}) custom-call(bf16[1,2,64,2048]{3,2,1,0:T(8,128)(2,1)S(1)} %get-tuple-element.13.gx_in, bf16[32,16,128]{2,1,0:T(8,128)(2,1)S(1)} %get-tuple-element.14.final1, ...), custom_call_target="tpu_custom_call" | custom-call | tf_op jit(solution)/shard_map/pallas_call | solution.py:656

commit v3 on v2

--- a/solution.py
+++ b/solution.py
@@ -44,7 +44,7 @@
     x_a, x_b, w1_ref, b1_ref, w2_ref, b2_ref, cot_ref,
     t1, t2, xf, xv, halo_a, halo_b, slope, pf, pool, halo_p, ps, pre_two, d2, gs_a, gs_b, gr_a, gr_b, gown,
     d1, d1t, xsend, xrecv, xown, outf,
-    acc1, half1, r11, r21,
+    half1, r11, r21,
     acc2, r02, half2, r12, r22,
     l_sem, s_send, s_recv, a_send, a_recv, z_send, z_recv, g_send, g_recv, c_send, c_recv, b_send, b_recv,
 ):
@@ -338,9 +338,13 @@
                 unit = (k * 3 + j) * 24 + part
                 acc2[unit // 7, pl.ds((unit % 7) * 8, 8), :] = s[part * 8:part * 8 + 8]
 
+    def all_of(src, dst, send, recv):
+        return pltpu.make_async_remote_copy(
+            src_ref=src, dst_ref=dst, send_sem=send, recv_sem=recv, device_id=partner, device_id_type=MESH)
+
     def swap_start(a, acc, r0):
         cp = pltpu.make_async_remote_copy(
-            src_ref=acc.at[pl.ds((1 - core) * 16, 16)], dst_ref=r0, send_sem=c_send.at[a, 0], recv_sem=c_recv.at[a, 0],
+            src_ref=acc.at[pl.ds((1 - core) * 16, 16)], dst_ref=r0, send_sem=c_send.at[0], recv_sem=c_recv.at[0],
             device_id=partner, device_id_type=MESH)
         cp.start()
         return cp
@@ -352,91 +356,69 @@
             half[i] = (acc[core * 16 + i] + r0[i]).astype(half.dtype)
             return carry
         lax.fori_loop(0, 16, add_half, 0)
-        sends = []
         for r in range(1, 16):
             da, db, q = chip_at(r)
-            cp = pltpu.make_async_remote_copy(
-                src_ref=half.at[q], dst_ref=r1.at[r - 1], send_sem=a_send.at[a, r - 1], recv_sem=a_recv.at[a, r - 1],
-                device_id=(da, db), device_id_type=MESH)
-            cp.start()
-            sends.append(cp)
-        return sends
+            pltpu.make_async_remote_copy(
+                src_ref=half.at[q], dst_ref=r1.at[r - 1], send_sem=a_send.at[0], recv_sem=a_recv.at[0],
+                device_id=(da, db), device_id_type=MESH).start()
+        return all_of(half.at[0:15], r1, a_send.at[0], a_recv.at[0])
 
     def column_start(a, sends, half, r1, r2):
         piece = half[chip + (core * 16 if a == 0 else 0)].astype(F32)
-        for r in range(len(sends)):
-            sends[r].wait()
+        sends.wait()
+        for r in range(r1.shape[0]):
             piece = piece + r1[r].astype(F32)
         r2[z] = piece.astype(r2.dtype)
-        sends = []
         for r in range(1, 8):
-            cp = pltpu.make_async_remote_copy(
-                src_ref=r2.at[z], dst_ref=r2.at[z], send_sem=z_send.at[a, r - 1], recv_sem=z_recv.at[a, r - 1],
-                device_id=z_at(r), device_id_type=MESH)
-            cp.start()
-            sends.append(cp)
-        return sends
+            pltpu.make_async_remote_copy(
+                src_ref=r2.at[z], dst_ref=r2.at[z], send_sem=z_send.at[a], recv_sem=z_recv.at[a],
+                device_id=z_at(r), device_id_type=MESH).start()
+        return all_of(r2.at[0:7], r2.at[0:7], z_send.at[a], z_recv.at[a])
 
     def gather_start(a, sends, r2, final):
-        for cp in sends:
-            cp.wait()
+        sends.wait()
         piece = r2[0].astype(F32)
         for i in range(1, 8):
             piece = piece + r2[i].astype(F32)
         mine = core * 16 + chip
         final[mine] = piece.astype(final.dtype)
-        sends = []
         for r in range(1, 16):
             da, db, q = chip_at(r)
-            cp = pltpu.make_async_remote_copy(
-                src_ref=final.at[mine], dst_ref=final.at[mine], send_sem=g_send.at[a, r - 1], recv_sem=g_recv.at[a, r - 1],
-                device_id=(da, db), device_id_type=MESH)
-            cp.start()
-            sends.append(cp)
-        return sends
+            pltpu.make_async_remote_copy(
+                src_ref=final.at[mine], dst_ref=final.at[mine], send_sem=g_send.at[0], recv_sem=g_recv.at[0],
+                device_id=(da, db), device_id_type=MESH).start()
+        return all_of(final.at[0:15], final.at[0:15], g_send.at[0], g_recv.at[0])
 
     def back_start(a, sends, final):
-        for cp in sends:
-            cp.wait()
+        sends.wait()
         cp = pltpu.make_async_remote_copy(
             src_ref=final.at[pl.ds(core * 16, 16)], dst_ref=final.at[pl.ds(core * 16, 16)],
-            send_sem=c_send.at[a, 1], recv_sem=c_recv.at[a, 1], device_id=partner, device_id_type=MESH)
+            send_sem=c_send.at[1], recv_sem=c_recv.at[1], device_id=partner, device_id_type=MESH)
         cp.start()
         return cp
 
     def scatter_start():
-        def convert(i, carry):
-            half1[i] = acc1[i].astype(half1.dtype)
-            return carry
-        lax.fori_loop(0, 32, convert, 0)
-        sends = []
         for r in range(31):
             da, db, q = chip_at(r + 1) if r < 15 else other_at(r - 15)
             owner = (core if r < 15 else 1 - core) * 16 + q
-            cp = pltpu.make_async_remote_copy(
-                src_ref=half1.at[owner], dst_ref=r11.at[r], send_sem=b_send.at[0, r], recv_sem=b_recv.at[0, r],
-                device_id=(da, db), device_id_type=MESH)
-            cp.start()
-            sends.append(cp)
-        return sends
+            pltpu.make_async_remote_copy(
+                src_ref=half1.at[owner], dst_ref=r11.at[r], send_sem=b_send.at[0], recv_sem=b_recv.at[0],
+                device_id=(da, db), device_id_type=MESH).start()
+        return all_of(half1.at[0:31], r11, b_send.at[0], b_recv.at[0])
 
     def spread_start(sends):
-        for cp in sends:
-            cp.wait()
+        sends.wait()
         piece = r21[0].astype(F32)
         for i in range(1, 8):
             piece = piece + r21[i].astype(F32)
         mine = core * 16 + chip
         fin1[mine] = piece.astype(fin1.dtype)
-        sends = []
         for r in range(31):
             da, db, q = chip_at(r + 1) if r < 15 else other_at(r - 15)
-            cp = pltpu.make_async_remote_copy(
-                src_ref=fin1.at[mine], dst_ref=fin1.at[mine], send_sem=b_send.at[1, r], recv_sem=b_recv.at[1, r],
-                device_id=(da, db), device_id_type=MESH)
-            cp.start()
-            sends.append(cp)
-        return sends
+            pltpu.make_async_remote_copy(
+                src_ref=fin1.at[mine], dst_ref=fin1.at[mine], send_sem=b_send.at[1], recv_sem=b_recv.at[1],
+                device_id=(da, db), device_id_type=MESH).start()
+        return all_of(fin1.at[0:31], fin1.at[0:31], b_send.at[1], b_recv.at[1])
 
     run2 = swap_start(1, acc2, r02)
 
@@ -473,10 +455,10 @@
 
     finish(g_pairs[0])
     carry = lax.fori_loop(
-        0, 7, functools.partial(delta_one, gr_a, 0), (jnp.zeros((32, 256), F32), pooled_tile(0, gr_a, 0)))
+        0, 7, functools.partial(delta_one, gr_a, 0), (jnp.zeros((32, 256), F32), pooled_tile(0, gr_a, 0)), unroll=True)
     finish(g_pairs[1])
     run2 = plane_start(1, run2, acc2, r02, half2, r12)
-    total_one, _ = lax.fori_loop(7, 16, functools.partial(delta_one, gr_b, 8), carry)
+    total_one, _ = lax.fori_loop(7, 16, functools.partial(delta_one, gr_b, 8), carry, unroll=True)
 
     def window_one(terms, q):
         lhs = jnp.concatenate([d1[d, BWD[q][j]] for d, k in terms for j in range(3)], axis=1)
@@ -517,9 +499,8 @@
         s = tap_one(tap)
         extra = pltpu.roll(last, 96 - 32 * tap, 1) if tap < 3 else total_col
         s = jnp.where(lane < 96, s, extra)
-        for part in range(8):
-            unit = tap * 8 + part
-            acc1[unit // 2, pl.ds((unit % 2) * 8, 8), :] = s[part * 8:part * 8 + 8]
+        for part in range(4):
+            half1[tap * 4 + part] = s[part * 16:part * 16 + 16].astype(LINK1)
     run1 = scatter_start()
 
     run2 = column_start(1, run2, half2, r12, r22)
@@ -534,8 +515,6 @@
     run1 = column_start(0, run1, half1, r11, r21)
     run2 = gather_start(1, run2, r22, fin2)
     run1 = spread_start(run1)
-    run2 = back_start(1, run2, fin2)
-
     for q in range(2):
         finish(x_pairs[q])
         for e in range(2):
@@ -553,9 +532,10 @@
         for t in range(16):
             gx_buf[0, e, :, t * 128:t * 128 + 128] = outf[e, t].astype(BF16)
 
+    run2 = back_start(1, run2, fin2)
+
     run2.wait()
-    for cp in run1:
-        cp.wait()
+    run1.wait()
 
 
 def unpack(scale_one, scale_two, gx_in, final1, final2, gx_ref, gw1_ref, gb1_ref, gw2_ref, gb2_ref):
@@ -616,7 +596,6 @@
         pltpu.VMEM((2, 2, 32, 2176), BF16),
         pltpu.VMEM((2, 2, 32, 2176), F32),
         pltpu.VMEM((2, 16, 64, 128), F32),
-        pltpu.VMEM((32, ROWS1, 128), F32),
         pltpu.VMEM((32, ROWS1, 128), LINK1),
         pltpu.VMEM((31, ROWS1, 128), LINK1),
         pltpu.VMEM((8, ROWS1, 128), LINK1),
@@ -628,16 +607,16 @@
         pltpu.SemaphoreType.DMA((7,)),
         pltpu.SemaphoreType.DMA((8, 2)),
         pltpu.SemaphoreType.DMA((8, 2)),
-        pltpu.SemaphoreType.DMA((2, 15)),
-        pltpu.SemaphoreType.DMA((2, 15)),
-        pltpu.SemaphoreType.DMA((2, 7)),
-        pltpu.SemaphoreType.DMA((2, 7)),
-        pltpu.SemaphoreType.DMA((2, 15)),
-        pltpu.SemaphoreType.DMA((2, 15)),
-        pltpu.SemaphoreType.DMA((2, 2)),
-        pltpu.SemaphoreType.DMA((2, 2)),
-        pltpu.SemaphoreType.DMA((2, 31)),
-        pltpu.SemaphoreType.DMA((2, 31)),
+        pltpu.SemaphoreType.DMA((1,)),
+        pltpu.SemaphoreType.DMA((1,)),
+        pltpu.SemaphoreType.DMA((2,)),
+        pltpu.SemaphoreType.DMA((2,)),
+        pltpu.SemaphoreType.DMA((1,)),
+        pltpu.SemaphoreType.DMA((1,)),
+        pltpu.SemaphoreType.DMA((2,)),
+        pltpu.SemaphoreType.DMA((2,)),
+        pltpu.SemaphoreType.DMA((2,)),
+        pltpu.SemaphoreType.DMA((2,)),
     ]
     gx, final1, final2 = pl.pallas_call(
         kernel,

time: 56.1 us -> 52.4 us (0.934)
  Pallas kernels: 55.4 us -> 51.7 us
    pallas_call x1, Pallas kernels: 54 us -> 50.3 us  [local(): pl.pallas_call(kernel, out_shape=(jax.ShapeDtypeStruct((1, 2, 64, 2048),...]
where the time goes in v3:
time: 52.4 us; the launch traced here: 52.3 us
  Pallas kernels  51.7 us (99%)
  between operations  0.64 us (1%)
    pallas_call x1, Pallas kernels, local(): pl.pallas_call(kernel, out_shape=(jax.ShapeDtypeStruct((1, 2, 64, 2048),...  50.3 us
    pallas_call x1, Pallas kernels, local(): pl.pallas_call(functools.partial(unpack, scale_one, scale_two), out_shape...  1.41 us

profile of v3, /device:TPU:1, one launch (start us, length us, event | category | flops | bytes accessed | tf_op | source)
XLA Modules:
  0.0 52.3 jit_solution(14626706524023101556)
XLA Ops:
  0.6 50.3 %shard_map.101 = (bf16[1,2,64,2048]{3,2,1,0:T(8,128)(2,1)S(1)}, bf16[32,16,128]{2,1,0:T(8,128)(2,1)S(1)}, bf16[32,56,128]{2,1,0:T(8,128)(2,1)S(1)}) custom-call(bf16[1,2,64,2048]{3,2,1,0:T(8,128)(2,1)} %x_hbm.1, bf16[3,3,3,32,64]{4,3,2,1,0:T(8,128)(2,1)} %w1_hbm.1, f32[1,64]{1,0:T(1,128)} %bitcast.4, bf16[3,3,3,64,128]{4,3,2,1,0:T(8,128)(2,1)} %w2_hbm.1, ...), custom_call_target="tpu_custom_call" | custom-call | tf_op jit(solution)/shard_map/pallas_call | solution.py:621
  50.9 1.4 %shard_map.102 = (bf16[1,2,64,2048]{3,2,1,0:T(8,128)(2,1)}, f32[3,3,3,32,64]{4,3,2,1,0:T(8,128)}, f32[1,64]{1,0:T(1,128)}, f32[3,3,3,64,128]{4,3,2,1,0:T(8,128)}, f32[1,128]{1,0:T(1,128)}) custom-call(bf16[1,2,64,2048]{3,2,1,0:T(8,128)(2,1)S(1)} %get-tuple-element.13.gx_in, bf16[32,16,128]{2,1,0:T(8,128)(2,1)S(1)} %get-tuple-element.14.final1, ...), custom_call_target="tpu_custom_call" | custom-call | tf_op jit(solution)/shard_map/pallas_call | solution.py:635

commit v4 on v3

--- a/solution.py
+++ b/solution.py
@@ -43,7 +43,7 @@
     gx_buf, fin1, fin2,
     x_a, x_b, w1_ref, b1_ref, w2_ref, b2_ref, cot_ref,
     t1, t2, xf, xv, halo_a, halo_b, slope, pf, pool, halo_p, ps, pre_two, d2, gs_a, gs_b, gr_a, gr_b, gown,
-    d1, d1t, xsend, xrecv, xown, outf,
+    d1, d1t, g_part, xsend, xrecv, xown, outf,
     half1, r11, r21,
     acc2, r02, half2, r12, r22,
     l_sem, s_send, s_recv, a_send, a_recv, z_send, z_recv, g_send, g_recv, c_send, c_recv, b_send, b_recv,
@@ -291,18 +291,17 @@
     carried = [None, None, None]
     done = 0
     for half in range(2):
-        if half == 0:
-            finish(p_pairs[0])
-            finish(p_pairs[1])
-        upto = (9, 17)[half]
+        finish(p_pairs[half])
+        upto = (8, 17)[half]
+        first, count = ((0, 7), (7, 9))[half]
         prepare_pool(halo_p.at[0], 0, done, upto)
         prepare_pool(halo_p.at[1], 2, done, upto)
         done = upto
-        pre = pre_two[pl.ds(half * 256, 256), :] + bias_two
-        pre = pre + dot(lhs_two((0, 2), half * 8, 8), jnp.concatenate([t2[0:768, :], t2[1536:2304, :]], axis=0))
+        pre = pre_two[pl.ds(first * 32, count * 32), :] + bias_two
+        pre = pre + dot(lhs_two((0, 2), first, count), jnp.concatenate([t2[0:768, :], t2[1536:2304, :]], axis=0))
         slp = slope_of(pre, sigmoid(pre))
-        for b in range(8):
-            block = half * 8 + b
+        for b in range(count):
+            block = first + b
             rows = pl.ds(block * 32, 32)
             delta = (cot_ref[0, 0, :, block * 256:block * 256 + 256].astype(F32) * slp[b * 32:b * 32 + 32]).astype(BF16)
             wide = delta.astype(F32)
@@ -310,16 +309,16 @@
             d2[0, rows, :] = shift_up(wide).astype(BF16)
             d2[2, rows, :] = shift_down(wide).astype(BF16)
             total_two = total_two + wide
-        rows = pl.ds(half * 256, 256)
+        rows = pl.ds(first * 32, count * 32)
         lhs = jnp.concatenate([d2[0, rows, :], d2[1, rows, :], d2[2, rows, :]], axis=1)
         for k in (0, 2):
             rhs = jnp.concatenate([t2[pl.ds((k * 3 + j) * 256, 256), :] for j in range(3)], axis=1)
             win = lax.dot_general(lhs, rhs, NT, preferred_element_type=F32)
 
             def put(t, piece, k=k):
-                ref, t = (gs_a, t) if t < 8 else (gs_b, t - 8)
+                ref, t = (gs_a, t) if t < 7 else (gs_b, t - 7)
                 ref[k // 2, :, t * 128:t * 128 + 128] = piece.astype(BF16)
-            carried[k] = window_tiles(win, half * 8, carried[k], put)
+            carried[k] = window_tiles(win, first, carried[k], put)
             if half == 1:
                 put(16, carried[k])
         put, got = ((gs_a, gr_a), (gs_b, gr_b))[half]
@@ -455,10 +454,47 @@
 
     finish(g_pairs[0])
     carry = lax.fori_loop(
-        0, 7, functools.partial(delta_one, gr_a, 0), (jnp.zeros((32, 256), F32), pooled_tile(0, gr_a, 0)), unroll=True)
+        0, 6, functools.partial(delta_one, gr_a, 0), (jnp.zeros((32, 256), F32), pooled_tile(0, gr_a, 0)), unroll=True)
+    def window_part(terms, q, first, count):
+        rows = pl.ds(first * 32, count * 32)
+        lhs = jnp.concatenate([d1[d, BWD[q][j], rows, :] for d, k in terms for j in range(3)], axis=1)
+        rhs = jnp.concatenate([t1[pl.ds((k * 3 + j) * 256, 256), :] for d, k in terms for j in range(3)], axis=1)
+        return lax.dot_general(lhs, rhs, NT, preferred_element_type=F32)
+
+    def turn(c):
+        for d in range(2):
+            for p in range(2):
+                v = d1[d, p, pl.ds(c * 128, 128), :]
+                d1t[:, pl.ds((d * 2 + p) * 512 + c * 128, 128)] = jnp.transpose(v)
+
+    def tap_dot(tap, first, last):
+        k, j = tap // 3, tap % 3
+        lhs = jnp.concatenate([
+            d1t[:, (d * 2 + p) * 512 + first * 32:(d * 2 + p) * 512 + last * 32]
+            for d in range(2) for p in range(2)], axis=1)
+        rhs = jnp.concatenate([
+            xv[d + k, FWD[p][j], :, b * 128:b * 128 + 256]
+            for d in range(2) for p in range(2) for b in range(first, last)], axis=0)
+        return dot(lhs, rhs)
+
+    def put_side(side, q):
+        def put(t, piece):
+            xsend[side, q, :, t * 128:t * 128 + 128] = piece.astype(BF16)
+        return put
+
+    turn(0)
+    for tap in range(9):
+        g_part[tap] = tap_dot(tap, 0, 4)
+    sides = (((0, 0),), ((1, 2),))
+    over = {}
+    for q in range(2):
+        for side in range(2):
+            win = window_part(sides[side], q, 0, 6)
+            over[side, q] = window_tiles(win, 0, None, put_side(side, q))
+
     finish(g_pairs[1])
     run2 = plane_start(1, run2, acc2, r02, half2, r12)
-    total_one, _ = lax.fori_loop(7, 16, functools.partial(delta_one, gr_b, 8), carry, unroll=True)
+    total_one, _ = lax.fori_loop(6, 16, functools.partial(delta_one, gr_b, 7), carry, unroll=True)
 
     def window_one(terms, q):
         lhs = jnp.concatenate([d1[d, BWD[q][j]] for d, k in terms for j in range(3)], axis=1)
@@ -467,16 +503,12 @@
 
     x_pairs = []
     for q in range(2):
-        for side, terms in ((0, ((0, 0),)), (1, ((1, 2),))):
-            def put(t, piece, side=side, q=q):
-                xsend[side, q, :, t * 128:t * 128 + 128] = piece.astype(BF16)
-            put(16, window_tiles(window_one(terms, q), 0, None, put))
+        for side in range(2):
+            put = put_side(side, q)
+            put(16, window_tiles(window_part(sides[side], q, 6, 10), 6, over[side, q], put))
         x_pairs.append(exchange(xsend.at[0, q], xsend.at[1, q], xrecv.at[1, q], xrecv.at[0, q], 6 + q))
-    for d in range(2):
-        for p in range(2):
-            for c in range(4):
-                v = d1[d, p, pl.ds(c * 128, 128), :]
-                d1t[:, pl.ds((d * 2 + p) * 512 + c * 128, 128)] = jnp.transpose(v)
+    for c in range(1, 4):
+        turn(c)
 
     total = jnp.sum(total_one, axis=0, keepdims=True)
     total = total[:, 0:128] + total[:, 128:256]
@@ -485,11 +517,7 @@
         jnp.where(lane == lax.broadcasted_iota(jnp.int32, (64, 128), 0), total, 0.0), axis=1, keepdims=True)
 
     def tap_one(tap):
-        k, j = tap // 3, tap % 3
-        rhs = jnp.concatenate([
-            xv[d + k, FWD[p][j], :, b * 128:b * 128 + 256]
-            for d in range(2) for p in range(2) for b in range(16)], axis=0)
-        g = dot(d1t[...], rhs)
+        g = g_part[tap] + tap_dot(tap, 4, 16)
         s = g[0:64, 0:128] + pltpu.roll(g[128:192, 0:128], 128 - 32, 1)
         s = s + pltpu.roll(g[64:128, 0:256], 256 - 64, 1)[:, 0:128]
         return s + pltpu.roll(g[192:256, 0:256], 256 - 96, 1)[:, 0:128]
@@ -585,13 +613,14 @@
         pltpu.VMEM((3, 3, 32, 2176), BF16),
         pltpu.VMEM((512, 256), F32),
         pltpu.VMEM((3, 512, 256), BF16),
-        pltpu.VMEM((2, 32, 1024), BF16),
-        pltpu.VMEM((2, 32, 1152), BF16),
-        pltpu.VMEM((2, 32, 1024), BF16),
-        pltpu.VMEM((2, 32, 1152), BF16),
+        pltpu.VMEM((2, 32, 896), BF16),
+        pltpu.VMEM((2, 32, 1280), BF16),
+        pltpu.VMEM((2, 32, 896), BF16),
+        pltpu.VMEM((2, 32, 1280), BF16),
         pltpu.VMEM((32, 2176), F32),
         pltpu.VMEM((2, 4, 512, 256), BF16),
         pltpu.VMEM((256, 2048), BF16),
+        pltpu.VMEM((9, 256, 256), F32),
         pltpu.VMEM((2, 2, 32, 2176), BF16),
         pltpu.VMEM((2, 2, 32, 2176), BF16),
         pltpu.VMEM((2, 2, 32, 2176), F32),

time: 52.4 us -> 50.9 us (0.971)
  Pallas kernels: 51.7 us -> 50.2 us
    pallas_call x1, Pallas kernels: 50.3 us -> 48.8 us  [local(): pl.pallas_call(kernel, out_shape=(jax.ShapeDtypeStruct((1, 2, 64, 2048),...]
where the time goes in v4:
time: 50.9 us; the launch traced here: 50.8 us
  Pallas kernels  50.2 us (99%)
  between operations  0.64 us (1%)
    pallas_call x1, Pallas kernels, local(): pl.pallas_call(kernel, out_shape=(jax.ShapeDtypeStruct((1, 2, 64, 2048),...  48.8 us
    pallas_call x1, Pallas kernels, local(): pl.pallas_call(functools.partial(unpack, scale_one, scale_two), out_shape...  1.41 us

profile of v4, /device:TPU:1, one launch (start us, length us, event | category | flops | bytes accessed | tf_op | source)
XLA Modules:
  0.0 50.8 jit_solution(16717409024076130105)
XLA Ops:
  0.6 48.8 %shard_map.101 = (bf16[1,2,64,2048]{3,2,1,0:T(8,128)(2,1)S(1)}, bf16[32,16,128]{2,1,0:T(8,128)(2,1)S(1)}, bf16[32,56,128]{2,1,0:T(8,128)(2,1)S(1)}) custom-call(bf16[1,2,64,2048]{3,2,1,0:T(8,128)(2,1)} %x_hbm.1, bf16[3,3,3,32,64]{4,3,2,1,0:T(8,128)(2,1)} %w1_hbm.1, f32[1,64]{1,0:T(1,128)} %bitcast.4, bf16[3,3,3,64,128]{4,3,2,1,0:T(8,128)(2,1)} %w2_hbm.1, ...), custom_call_target="tpu_custom_call" | custom-call | tf_op jit(solution)/shard_map/pallas_call | solution.py:650
  49.4 1.4 %shard_map.102 = (bf16[1,2,64,2048]{3,2,1,0:T(8,128)(2,1)}, f32[3,3,3,32,64]{4,3,2,1,0:T(8,128)}, f32[1,64]{1,0:T(1,128)}, f32[3,3,3,64,128]{4,3,2,1,0:T(8,128)}, f32[1,128]{1,0:T(1,128)}) custom-call(bf16[1,2,64,2048]{3,2,1,0:T(8,128)(2,1)S(1)} %get-tuple-element.13.gx_in, bf16[32,16,128]{2,1,0:T(8,128)(2,1)S(1)} %get-tuple-element.14.final1, ...), custom_call_target="tpu_custom_call" | custom-call | tf_op jit(solution)/shard_map/pallas_call | solution.py:664
